TPU v7x, 64 devices: a 2x2x8 block of a 4x4x8 slice. The times are simulated.
64 devices in a mesh: dp: 4 (over x, y), tp: 16 (over z, core).
Axes of the slice: x: 2, y: 2, z: 8, core: 2. Of those that a mesh axis runs over, the one named last changes fastest.
The devices are a block of a 4x4x8 slice.
Arguments:
- x_rows: bfloat16 [32768, 4096], P(('dp', 'tp')), parts along dimension 0
- norm_gain: float32 [4096], replicated
- w_q: bfloat16 [4096, 32, 128], P(None, 'tp')
- w_k: bfloat16 [4096, 1024], P(None, 'tp')
- w_v: bfloat16 [4096, 1024], P(None, 'tp')
Outputs:
- output 1: bfloat16 [32768, 32, 128], P('dp', 'tp'), parts along dimension 0
- output 2: bfloat16 [32768, 16, 128], P('dp', 'tp'), parts along dimension 0
- output 3: bfloat16 [32768, 16, 128], P('dp', 'tp'), parts along dimension 0
There are 4 independent parts. A program takes and returns all parts, laid end to end along the dimension named above; an argument that names none is the same for every part.
All inputs are finite; a program needn't handle non-finite values.
Results may differ from a plain program's by a relative error of at most 0.001.
Values are sent between devices in bfloat16 or wider.
A program may use at most 768 MiB of HBM per device.

v0:
```python
import jax
import jax.numpy as jnp
from jax import lax
from jax.sharding import PartitionSpec as P

EPSILON = 1e-6


def solution(mesh):
    group_size = mesh.shape["tp"]

    def head_pieces(piece, head_share):
        member = lax.axis_index("tp") % head_share
        received = [piece]
        for step_ahead in range(1, head_share):
            send_pairs = [(source, (source // head_share) * head_share + (source % head_share - step_ahead) % head_share) for source in range(group_size)]
            received.append(lax.ppermute(piece, "tp", send_pairs))
        joined = jnp.concatenate(received, axis=1)
        return jnp.roll(joined, member * piece.shape[1], axis=1)

    def local_step(x_rows, norm_gain, w_q, w_k, w_v):
        x_wide = x_rows.astype(jnp.float32)
        mean_sq = jnp.mean(x_wide * x_wide, axis=-1, keepdims=True)
        normed = (x_wide * lax.rsqrt(mean_sq + EPSILON) * norm_gain).astype(jnp.bfloat16)
        gathered = lax.all_gather(normed, "tp", axis=0, tiled=True)
        q_local = jnp.einsum("td,dhe->the", gathered, w_q, preferred_element_type=jnp.float32).astype(jnp.bfloat16)
        k_piece = jnp.dot(gathered, w_k, preferred_element_type=jnp.float32).astype(jnp.bfloat16)
        v_piece = jnp.dot(gathered, w_v, preferred_element_type=jnp.float32).astype(jnp.bfloat16)
        head_share = w_q.shape[2] // w_k.shape[1]
        k_head = head_pieces(k_piece, head_share)
        v_head = head_pieces(v_piece, head_share)
        return q_local, k_head[:, None, :], v_head[:, None, :]

    return jax.shard_map(local_step, mesh=mesh, in_specs=(P(("dp", "tp"), None), P(None), P(None, "tp", None), P(None, "tp"), P(None, "tp")), out_specs=(P("dp", "tp", None), P("dp", "tp", None), P("dp", "tp", None)), check_vma=False)
```

profile of v0, /device:TPU:22, one launch (start us, length us, event | category | flops | bytes accessed | tf_op | source)
XLA Modules:
  0.0 469.4 jit_solution(1908637079436586702)
XLA Ops:
  7.2 0.0 copy-start
  7.2 0.1 all-gather.2.cloned.1.call-start
  7.3 0.0 copy-start.1
  7.3 3.2 fusion.5
  10.5 0.3 copy-done.1
  10.8 4.4 fusion.7
  15.2 0.0 copy-start.2
  15.2 0.1 all-gather.2.cloned.1.call-update
  15.3 332.9 %all-gather.2.cloned.1.call-done = bf16[8192,4096]{1,0:T(8,128)(2,1)} async-done(((bf16[512,4096]{1,0:T(8,128)(2,1)}), bf16[8192,4096]{1,0:T(8,128)(2,1)}) %all-gather.2.cloned.1.call-update) | async-done | bytes 67108880 | tf_op jit(solution)/shard_map/all_gather | solution.py:25
  348.2 0.0 copy-done.2
  348.2 28.3 %convolution_convert_fusion.1 = bf16[8192,64]{0,1:T(8,128)(2,1)} fusion(bf16[8192,4096]{1,0:T(8,128)(2,1)} %all-gather.2.cloned.1.call-done, bf16[4096,64]{0,1:T(8,128)(2,1)S(1)} %copy-done.2), kind=kOutput, calls=%fused_computation.6 | convolution fusion | flops 4295491584 | bytes 68681728 | tf_op jit(solution)/shard_map/dot_general | solution.py:27
  376.5 0.2 collective-permute-start
  376.8 28.9 %convolution_convert_fusion = bf16[8192,64]{0,1:T(8,128)(2,1)S(1)} fusion(bf16[8192,4096]{1,0:T(8,128)(2,1)} %all-gather.2.cloned.1.call-done, bf16[4096,64]{0,1:T(8,128)(2,1)} %param.11), kind=kOutput, calls=%fused_computation.5 | convolution fusion | flops 4295491584 | bytes 68681728 | tf_op jit(solution)/shard_map/dot_general | solution.py:28
  405.7 0.6 collective-permute-start.1
  406.2 0.0 copy-done
  406.2 28.3 %fusion.2 = bf16[8192,2,128]{2,0,1:T(8,128)(2,1)} fusion(bf16[8192,4096]{1,0:T(8,128)(2,1)} %all-gather.2.cloned.1.call-done, bf16[4096,2,128]{2,1,0:T(2,128)(2,1)S(1)} %copy-done), kind=kOutput, calls=%fused_computation.4 | convolution fusion | flops 17181966336 | bytes 73400320 | tf_op jit(solution)/shard_map/td,dhe->the/dot_general | solution.py:26
  434.6 10.1 %copy.13 = bf16[8192,2,128]{2,1,0:T(2,128)(2,1)} copy(bf16[8192,2,128]{2,0,1:T(8,128)(2,1)} %fusion.2) | data formatting | bytes 8388608
  444.7 0.0 collective-permute-done
  444.7 5.1 %fusion.12 = bf16[8192,128]{0,1:T(8,128)(2,1)} fusion(s32[]{:T(128)S(6)} %select_n.22, bf16[8192,64]{0,1:T(8,128)(2,1)} %convolution_convert_fusion.1, bf16[8192,64]{0,1:T(8,128)(2,1)} %collective-permute-done), kind=kLoop, calls=%fused_computation.22 | loop fusion | flops 8388608 | bytes 4194308 | tf_op jit(solution)/shard_map/jit(_roll_dynamic)/concatenate | solution.py:19
  449.8 4.1 copy.11
  453.9 0.0 collective-permute-done.1
  453.9 4.6 fusion.9
  458.5 4.1 copy.12
  (1 shorter events, 0.0 us)
Async XLA Ops:
  7.2 399.1 %copy-start = (bf16[4096,2,128]{2,1,0:T(2,128)(2,1)S(1)}, bf16[4096,2,128]{2,1,0:T(2,128)(2,1)}, u32[]{:S(2)}) copy-start(bf16[4096,2,128]{2,1,0:T(2,128)(2,1)} %param.9) | copy-start | bytes 6291460
  7.2 341.0 %all-gather.2.cloned.1.call-start = ((), (), s32[]{:S(2)}) async-start(), calls=%async_computation | async-start | bytes 71303168 | tf_op jit(solution)/shard_map/all_gather | solution.py:25
  7.3 3.6 copy-start.1
  15.2 333.0 %copy-start.2 = (bf16[4096,64]{0,1:T(8,128)(2,1)S(1)}, bf16[4096,64]{0,1:T(8,128)(2,1)}, u32[]{:S(2)}) copy-start(bf16[4096,64]{0,1:T(8,128)(2,1)} %param.10) | copy-start | bytes 1572868
  376.5 68.2 %collective-permute-start = (bf16[8192,64]{0,1:T(8,128)(2,1)}, bf16[8192,64]{0,1:T(8,128)(2,1)}, u32[]{:S(2)}, u32[]{:S(2)}) collective-permute-start(bf16[8192,64]{0,1:T(8,128)(2,1)} %convolution_convert_fusion.1), channel_id=1, source_target_pairs={{0,1},{1,0},{2,3},{3,2},{4,5},{5,4},{6,7},{7,6},{8,9},{9,8},{10,11... | collective-permute-start | bytes 3145736 | tf_op jit(solution)/shard_map/ppermute | solution.py:17
  405.7 48.2 %collective-permute-start.1 = (bf16[8192,64]{0,1:T(8,128)(2,1)S(1)}, bf16[8192,64]{0,1:T(8,128)(2,1)}, u32[]{:S(2)}, u32[]{:S(2)}) collective-permute-start(bf16[8192,64]{0,1:T(8,128)(2,1)S(1)} %convolution_convert_fusion), channel_id=1, source_target_pairs={{0,1},{1,0},{2,3},{3,2},{4,5},{5,4},{6,7},{7,6},{8,9},{9,8},{10,11... | collective-permute-start | bytes 3145736 | tf_op jit(solution)/shard_map/ppermute | solution.py:17
Sparse Core Ops, SparseCore 0:
  15.4 332.7 all-gather.1
where the time goes:
time: 471 us; the launch traced here: 469 us
  waiting for transfers between devices  333 us (71%)
  matrix products  85.6 us (18%)
  local copies, waits for them, and re-layouts  18.6 us (4%)
  other arithmetic  17.4 us (4%)
  between operations  14.1 us (3%)
    all_gather x1, waiting for transfers between devices, local_step(): gathered = lax.all_gather(normed, 'tp', axis=0, tiled=True)  333 us
    dot_general x1, matrix products, local_step(): jnp.dot(gathered, w_v, preferred_element_type=jnp.float32)  28.9 us
    dot_general x1, matrix products, local_step(): jnp.einsum('td,dhe->the', gathered, w_q, preferred_element_type=jnp.float32)  28.3 us
    dot_general x1, matrix products, local_step(): jnp.dot(gathered, w_k, preferred_element_type=jnp.float32)  28.3 us
    unnamed x7, local copies, waits for them, and re-layouts  10.4 us
    concatenate x2, other arithmetic, head_pieces(): return jnp.roll(joined, member * piece.shape[1], axis=1)  9.76 us
  transfers between devices with their start and end apart: 3, of which 1 were waited for; matrix products, arithmetic and copies ran while one was open for 16% of the time, Pallas kernels for 0%

commit v1 on v0

v1 whole, which is shorter than its diff:
```python
import functools
import math

import jax
import jax.numpy as jnp
from jax import lax
from jax.experimental import pallas as pl
from jax.experimental.pallas import tpu as pltpu
from jax.sharding import PartitionSpec as P

EPSILON = 1e-6
MESH = pl.DeviceIdType.MESH
CORES = 2
QUARTERS = 4
HALVES = 2
CHUNKS = QUARTERS * HALVES
TILE = 256
NORM_ROWS = 16
ORDER = (7, 2, 6, 4, 3, 5, 1)


def kernel(ring, side, x_hbm, gain_hbm, wq_hbm, wk_hbm, wv_hbm, q_out, kv_out,
           rows, gain, wq, wkv, wflat, oq, okv,
           local_sem, x_send, x_recv, pair_send, pair_recv, z_send, z_recv, xy_send, xy_recv,
           oq_send, okv_send, oq_recv, okv_recv, fw_send, fw_recv, keep_sem):
    dp, tp = lax.axis_index("dp"), lax.axis_index("tp")
    z, c = tp // CORES, tp % CORES
    grid_x, grid_y = dp // side, dp % side
    odd_x, odd_y = grid_x % 2, grid_y % 2
    quarter = 2 * odd_x + odd_y
    quarter_x, quarter_y, quarter_d = 2 * (1 - odd_x) + odd_y, 2 * odd_x + 1 - odd_y, 3 - quarter
    x_peer = (dp + side * (1 - 2 * odd_x), tp)
    y_peer = (dp + 1 - 2 * odd_y, tp)
    partner = (dp, tp + 1 - 2 * c)

    own, depth = x_hbm.shape
    chip_rows = CORES * own
    step = depth // CHUNKS
    piece = wk_hbm.shape[0]
    tiles = chip_rows // TILE

    def at_ring(distance):
        return (dp, CORES * ((z + ring - distance) % ring) + c)

    def remote(src, dst, send, recv, device):
        return pltpu.make_async_remote_copy(src_ref=src, dst_ref=dst, send_sem=send, recv_sem=recv, device_id=device, device_id_type=MESH)

    def part(block, chunk):
        first = pl.multiple_of(chunk * step, step)
        return wq.at[block, pl.ds(first, step)], wkv.at[block, chunk]

    own_first = pl.multiple_of(c * own, own)
    lane = own // 4
    x_loads = [pltpu.make_async_copy(x_hbm.at[pl.ds(i * lane, lane)], rows.at[pl.ds(own_first + i * lane, lane)], local_sem.at[i]) for i in range(4)]
    w_loads = []
    for i in range(QUARTERS):
        first = pl.multiple_of(((quarter + i) % QUARTERS) * (depth // QUARTERS), depth // QUARTERS)
        w_loads.append(pltpu.make_async_copy(wq_hbm.at[pl.ds(first, depth // QUARTERS)], wq.at[z, pl.ds(first, depth // QUARTERS)], local_sem.at[4 + i]))
    gain_load = pltpu.make_async_copy(gain_hbm, gain, local_sem.at[8])
    own_half = pl.ds(pl.multiple_of(c * piece, piece), piece)

    def columns(i):
        chunk = (HALVES * quarter + i) % CHUNKS
        return chunk, pl.ds(pl.multiple_of(chunk * step, step), step)

    def pair_load(source, i):
        chunk, span = columns(i)
        return pltpu.make_async_copy(source.at[:, span], wkv.at[z, chunk, own_half], local_sem.at[9 + i])

    def pair_copy(source, i):
        chunk, span = columns(i)
        return remote(source.at[:, span], wkv.at[z, chunk, own_half], pair_send.at[i], pair_recv.at[i], partner)

    def pair_arrival(i):
        chunk, span = columns(i)
        other_half = pl.ds(pl.multiple_of((1 - c) * piece, piece), piece)
        return remote(wk_hbm.at[:, span], wkv.at[z, chunk, other_half], pair_send.at[i], pair_recv.at[i], partner)

    w_loads[0].start()
    for load in x_loads:
        load.start()
    gain_load.start()

    @pl.when(c == 0)
    def _():
        for i in range(CHUNKS):
            pair_load(wk_hbm, i).start()

    @pl.when(c == 1)
    def _():
        for i in range(CHUNKS):
            pair_load(wv_hbm, i).start()

    for load in w_loads[1:]:
        load.start()

    barrier = pltpu.get_barrier_semaphore()
    peers = [x_peer, y_peer, partner] + [at_ring(r) for r in range(1, ring)]
    for peer in peers:
        pl.semaphore_signal(barrier, inc=1, device_id=peer, device_id_type=MESH)
    pl.semaphore_wait(barrier, len(peers))

    @pl.when(c == 0)
    def _():
        for i in range(CHUNKS):
            pair_copy(wv_hbm, i).start()

    @pl.when(c == 1)
    def _():
        for i in range(CHUNKS):
            pair_copy(wk_hbm, i).start()

    half_ring = ring // 2
    started = []

    def ring_send(direction, hop, half, kind):
        back = hop if direction == 0 else ring - hop
        block = (z + ring - back) % ring
        reference = part(block, HALVES * quarter + half)[kind]
        index = ((back * HALVES + half) * 2 + kind) if hop else ((direction * ring * HALVES + half) * 2 + kind)
        landed = (hop + 1) if direction == 0 else ring - hop - 1
        copy = remote(reference, reference, z_send.at[index], z_recv.at[(landed * HALVES + half) * 2 + kind], at_ring(ring - 1 if direction == 0 else 1))
        copy.start()
        started.append(copy)

    def reach(direction, half):
        return half_ring if direction == half else half_ring - 1

    def ring_arrival(direction, hop, half, kind):
        back = hop if direction == 0 else ring - hop
        block = (z + ring - back) % ring
        reference = part(block, HALVES * quarter + half)[kind]
        remote(reference, reference, z_send.at[0], z_recv.at[(back * HALVES + half) * 2 + kind], at_ring(1)).wait_recv()

    def ring_service(hop, half):
        for kind in range(2):
            for direction in range(2):
                if hop <= reach(direction, half):
                    ring_arrival(direction, hop, half, kind)
                    if hop < reach(direction, half):
                        ring_send(direction, hop, half, kind)

    def square_copy(r, lane_index, chunk, kind, device):
        block = (z + ring - r) % ring
        reference = part(block, chunk)[kind]
        index = (r * 6 + lane_index) * 2 + kind
        return remote(reference, reference, xy_send.at[index], xy_recv.at[index], device)

    def square_send(r, half):
        for kind in range(2):
            for base, device in ((0, x_peer), (2, y_peer)):
                copy = square_copy(r, base + half, HALVES * quarter + half, kind, device)
                copy.start()
                started.append(copy)

    def square_forward(r, half):
        base, chunk, device = ((0, HALVES * quarter_x, y_peer), (2, HALVES * quarter_y, x_peer))[half]
        for kind in range(2):
            square_copy(r, base + half, chunk + half, kind, device).wait_recv()
            copy = square_copy(r, 4 + half, chunk + half, kind, device)
            copy.start()
            started.append(copy)

    def square_rest(r):
        for kind in range(2):
            square_copy(r, 1, HALVES * quarter_x + 1, kind, x_peer).wait_recv()
            square_copy(r, 2, HALVES * quarter_y, kind, y_peer).wait_recv()
            square_copy(r, 4, HALVES * quarter_d, kind, y_peer).wait_recv()
            square_copy(r, 5, HALVES * quarter_d + 1, kind, x_peer).wait_recv()

    def flatten(block):
        @pl.loop(0, CHUNKS)
        def _(i):
            span = pl.ds(pl.multiple_of(i * step, step), step)
            wflat[span, :] = wq[block, span].reshape(step, wflat.shape[1])

    def product(block, slot, first):
        span = pl.ds(first, TILE)
        q = jnp.dot(rows[span, :], wflat[...], preferred_element_type=jnp.float32)
        oq[slot, span] = q.reshape((TILE,) + oq.shape[2:]).astype(oq.dtype)
        kv = jnp.zeros((TILE, okv.shape[2]), jnp.float32)
        for i in range(CHUNKS):
            kv += lax.dot_general(rows[span, pl.ds(i * step, step)], wkv[block, i], (((1,), (1,)), ((), ())), preferred_element_type=jnp.float32)
        okv[slot, span] = kv.astype(okv.dtype)

    def out_rows(block, first, count):
        return pl.ds(pl.multiple_of(block * chip_rows + first, TILE), count)

    def out_copies(r, first, count):
        span, target = pl.ds(first, count), out_rows(z, first, count)
        return (
            remote(oq.at[r, span], q_out.at[target], oq_send.at[r], oq_recv.at[r], at_ring(r)),
            remote(okv.at[r, span], kv_out.at[c, target], okv_send.at[r], okv_recv.at[r], at_ring(r)),
        )

    def multiply(r):
        block = (z + ring - r) % ring
        flatten(block)

        @pl.loop(0, tiles)
        def _(t):
            first = pl.multiple_of(t * TILE, TILE)
            product(block, r, first)
            for copy in out_copies(r, first, TILE):
                copy.start()

    def keep_copies():
        target = out_rows(z, 0, chip_rows)
        return (
            pltpu.make_async_copy(oq.at[0], q_out.at[target], keep_sem.at[0]),
            pltpu.make_async_copy(okv.at[0], kv_out.at[c, target], keep_sem.at[1]),
        )

    def hand_over(r, source):
        target = out_rows((z + r) % ring, 0, chip_rows)
        return remote(source, kv_out.at[c, target], fw_send.at[r], fw_recv.at[r], partner)

    def hand_arrival(r):
        target = out_rows((z + r) % ring, 0, chip_rows)
        return remote(okv.at[0], kv_out.at[1 - c, target], fw_send.at[r], fw_recv.at[r], partner)

    def relay(r):
        target = out_rows((z + r) % ring, 0, chip_rows)
        remote(okv.at[r], kv_out.at[c, target], okv_send.at[r], okv_recv.at[r], at_ring(r)).wait_recv()
        hand_over(r, kv_out.at[c, target]).start()

    w_loads[0].wait()
    for half in range(HALVES):
        for direction in range(2):
            ring_send(direction, 0, half, 0)
    for i in range(CHUNKS):
        pair_load(wk_hbm, i).wait()
    for half in range(HALVES):
        pair_arrival(half).wait_recv()
        for direction in range(2):
            ring_send(direction, 0, half, 1)

    gain_load.wait()
    for i in range(4):
        x_loads[i].wait()

        @pl.loop(0, lane // NORM_ROWS)
        def _(n):
            span = pl.ds(pl.multiple_of(own_first + i * lane + n * NORM_ROWS, NORM_ROWS), NORM_ROWS)
            wide = rows[span, :].astype(jnp.float32)
            mean_sq = jnp.mean(wide * wide, axis=-1, keepdims=True)
            rows[span, :] = (wide * lax.rsqrt(mean_sq + EPSILON) * gain[...]).astype(rows.dtype)

        span = pl.ds(own_first + i * lane, lane)
        remote(rows.at[span], rows.at[span], x_send.at[i], x_recv.at[i], partner).start()

    ring_service(1, 0)
    square_send(ORDER[0], 0)

    for i in range(4):
        span = pl.ds(pl.multiple_of((1 - c) * own + i * lane, lane), lane)
        remote(rows.at[span], rows.at[span], x_send.at[i], x_recv.at[i], partner).wait_recv()
    for load in w_loads[1:]:
        load.wait()
    for i in range(HALVES, CHUNKS):
        pair_arrival(i).wait_recv()
    flatten(z)

    def own_products(first_tile, count):
        @pl.loop(first_tile, first_tile + count)
        def _(t):
            product(z, 0, pl.multiple_of(t * TILE, TILE))

    own_products(0, tiles // 2)
    ring_service(1, 1)
    square_send(ORDER[0], 1)
    own_products(tiles // 2, tiles - tiles // 2)
    for copy in keep_copies():
        copy.start()
    hand_over(0, okv.at[0]).start()
    square_forward(ORDER[0], 0)
    ring_service(2, 0)
    square_send(ORDER[1], 0)

    services = {(0, 0): ((2, 1),), (0, 1): ((3, 0),), (1, 0): ((3, 1),), (1, 1): ((4, 0),), (2, 0): ((4, 1),)}
    blocks = len(ORDER)
    for j in range(blocks):
        square_forward(ORDER[j], 1)
        for hop, half in services.get((j, 0), ()):
            ring_service(hop, half)
        if j + 1 < blocks:
            square_send(ORDER[j + 1], 1)
            square_forward(ORDER[j + 1], 0)
        for hop, half in services.get((j, 1), ()):
            ring_service(hop, half)
        if j + 2 < blocks:
            square_send(ORDER[j + 2], 0)
        square_rest(ORDER[j])
        multiply(ORDER[j])
        if j >= 3:
            relay(ORDER[j - 3])

    for r in ORDER[blocks - 3:]:
        relay(r)
    for r in ORDER:
        target = out_rows((z + r) % ring, 0, chip_rows)
        remote(oq.at[r], q_out.at[target], oq_send.at[r], oq_recv.at[r], at_ring(r)).wait_recv()
    for r in range(ring):
        hand_arrival(r).wait_recv()

    for copy in keep_copies():
        copy.wait()
    for copy in started:
        copy.wait_send()
    for r in ORDER:
        for copy in out_copies(r, 0, chip_rows):
            copy.wait_send()
    for r in range(ring):
        hand_over(r, okv.at[0]).wait_send()
    for i in range(4):
        span = pl.ds(own_first + i * lane, lane)
        remote(rows.at[span], rows.at[span], x_send.at[i], x_recv.at[i], partner).wait_send()
    for i in range(CHUNKS):
        pair_copy(wk_hbm, i).wait_send()


def solution(mesh):
    ring = mesh.shape["tp"] // CORES
    side = math.isqrt(mesh.shape["dp"])
    assert side * side == mesh.shape["dp"] and side % 2 == 0

    def local_step(x_rows, norm_gain, w_q, w_k, w_v):
        own, depth = x_rows.shape
        heads, width = w_q.shape[1:]
        piece = w_k.shape[1]
        assert piece * CORES == width
        tokens, chip_rows, step = own * CORES * ring, own * CORES, depth // CHUNKS
        dma = pltpu.SemaphoreType.DMA
        bf16 = x_rows.dtype
        q_out, kv_out = pl.pallas_call(
            functools.partial(kernel, ring, side),
            out_shape=(
                jax.ShapeDtypeStruct((tokens, heads, width), bf16),
                jax.ShapeDtypeStruct((CORES, tokens, width), bf16),
            ),
            in_specs=[pl.BlockSpec(memory_space=pl.ANY)] * 5,
            out_specs=(pl.BlockSpec(memory_space=pl.ANY),) * 2,
            scratch_shapes=[
                pltpu.VMEM((chip_rows, depth), bf16),
                pltpu.VMEM((1, depth), jnp.float32),
                pltpu.VMEM((ring, depth, heads, width), bf16),
                pltpu.VMEM((ring, CHUNKS, width, step), bf16),
                pltpu.VMEM((depth, heads * width), bf16),
                pltpu.VMEM((ring, chip_rows, heads, width), bf16),
                pltpu.VMEM((ring, chip_rows, width), bf16),
                dma((9 + CHUNKS,)),
                dma((4,)), dma((4,)),
                dma((CHUNKS,)), dma((CHUNKS,)),
                dma((2 * ring * HALVES * 2,)), dma((ring * HALVES * 2,)),
                dma((ring * 6 * 2,)), dma((ring * 6 * 2,)),
                dma((ring,)), dma((ring,)), dma((ring,)), dma((ring,)),
                dma((ring,)), dma((ring,)),
                dma((2,)),
            ],
            compiler_params=pltpu.CompilerParams(collective_id=0, has_side_effects=True, vmem_limit_bytes=56 * 1024 * 1024),
        )(x_rows, norm_gain.reshape(1, depth), w_q, w_k.T, w_v.T)
        return q_out, kv_out[0][:, None, :], kv_out[1][:, None, :]

    return jax.shard_map(local_step, mesh=mesh, in_specs=(P(("dp", "tp"), None), P(None), P(None, "tp", None), P(None, "tp"), P(None, "tp")), out_specs=(P("dp", "tp", None), P("dp", "tp", None), P("dp", "tp", None)), check_vma=False)
```

time: 471 us -> 254 us (0.54)
  waiting for transfers between devices: 333 us -> 0 us
  Pallas kernels: 0 us -> 244 us
  matrix products: 85.6 us -> 0 us
  other arithmetic: 17.4 us -> 0 us
  between operations: 14.1 us -> 0.65 us
  local copies, waits for them, and re-layouts: 18.6 us -> 6.67 us
    all_gather x1 -> x0, waiting for transfers between devices: 333 us -> none  [local_step(): gathered = lax.all_gather(normed, 'tp', axis=0, tiled=True)]
    pallas_call x0 -> x1, Pallas kernels: none -> 244 us  [local_step(): pl.pallas_call(functools.partial(kernel, ring, side), out_shape=(jax.Shap...]
    dot_general x3 -> x0, matrix products: 85.6 us -> none  [the longest x1 28.9 us: local_step(): jnp.dot(gathered, w_v, preferred_element_type=jnp.float32)]
    concatenate x2 -> x0, other arithmetic: 9.76 us -> none  [head_pieces(): return jnp.roll(joined, member * piece.shape[1], axis=1)]
    unnamed x7 -> x3, local copies, waits for them, and re-layouts: 10.4 us -> 2.02 us
    dynamic_slice x2 -> x0, local copies, waits for them, and re-layouts: 8.12 us -> none  [head_pieces(): return jnp.roll(joined, member * piece.shape[1], axis=1)]
  transfers between devices with their start and end apart: 3 -> 0, of which waited for: 1 -> 0; matrix products, arithmetic and copies ran while one was open for 16% -> 0% of each run, Pallas kernels for 0% -> 0%
where the time goes in v1:
time: 254 us; the launch traced here: 252 us
  Pallas kernels  244 us (96%)
  local copies, waits for them, and re-layouts  6.67 us (3%)
    pallas_call x1, Pallas kernels, local_step(): pl.pallas_call(functools.partial(kernel, ring, side), out_shape=(jax.Shap...  244 us

profile of v1, /device:TPU:22, one launch (start us, length us, event | category | flops | bytes accessed | tf_op | source)
XLA Modules:
  0.0 251.5 jit_solution(3139965262066692224)
XLA Ops:
  0.6 244.2 %shard_map.76 = (bf16[8192,2,128]{2,1,0:T(2,128)(2,1)}, bf16[2,8192,128]{2,1,0:T(8,128)(2,1)}) custom-call(bf16[512,4096]{1,0:T(8,128)(2,1)} %x_hbm.1, f32[1,4096]{1,0:T(1,128)} %bitcast.9, bf16[4096,2,128]{2,1,0:T(2,128)(2,1)} %wq_hbm.1, bf16[64,4096]{1,0:T(8,128)(2,1)} %bitcast.7, bf16[64,4096]{1,0:T(8,128)(2,1)} %bitcast.8), custom_call_target="tpu_custom_call" | custom-call | tf_op jit(solution)/shard_map/pallas_call | solution.py:335
  244.8 0.0 copy-start
  244.8 4.7 %slice_bitcast_fusion = (bf16[8192,1,128]{2,0,1:T(8,128)(2,1)}, bf16[8192,1,128]{2,0,1:T(8,128)(2,1)}) fusion(bf16[2,8192,128]{2,1,0:T(8,128)(2,1)} %get-tuple-element.6), kind=kLoop, calls=%fused_computation | loop fusion | bytes 8388608 | tf_op jit(solution)/shard_map/broadcast_in_dim;squeeze | solution.py:362
  249.5 0.0 copy-done
  249.5 2.0 copy.9
Async XLA Ops:
  244.8 4.7 %copy-start = (bf16[8192,2,128]{2,1,0:T(2,128)(2,1)S(1)}, bf16[8192,2,128]{2,1,0:T(2,128)(2,1)}, u32[]{:S(2)}) copy-start(bf16[8192,2,128]{2,1,0:T(2,128)(2,1)} %get-tuple-element.12) | copy-start | bytes 12582916

commit v2 on v1

--- a/solution.py
+++ b/solution.py
@@ -16,7 +16,30 @@
 CHUNKS = QUARTERS * HALVES
 TILE = 256
 NORM_ROWS = 16
-ORDER = (7, 2, 6, 4, 3, 5, 1)
+
+ARRIVE, SPREAD, FORWARD, MULTIPLY, HAND_OVER, NORM, OWN = range(7)
+SCHEDULE = (
+    (NORM, 0, 0, 0), (NORM, 0, 0, 0), (NORM, 0, 0, 0), (ARRIVE, 1, 1, 0), (SPREAD, 7, 1, 0),
+    (NORM, 0, 0, 0), (OWN, 0, 1, 0), (ARRIVE, 1, 1, 1), (SPREAD, 7, 1, 1), (SPREAD, 1, 1, 0),
+    (SPREAD, 1, 1, 1), (OWN, 0, 0, 0), (ARRIVE, 1, 0, 0), (FORWARD, 7, 1, 0), (FORWARD, 7, 1, 1),
+    (FORWARD, 1, 1, 0), (ARRIVE, 1, 0, 1), (FORWARD, 1, 1, 1), (ARRIVE, 2, 1, 0), (SPREAD, 2, 1, 0),
+    (MULTIPLY, 7, 1, 0), (ARRIVE, 2, 1, 1), (SPREAD, 2, 1, 1), (MULTIPLY, 1, 1, 0), (ARRIVE, 2, 0, 0),
+    (FORWARD, 2, 1, 0), (SPREAD, 2, 0, 0), (FORWARD, 2, 1, 1), (ARRIVE, 2, 0, 1), (SPREAD, 2, 0, 1),
+    (SPREAD, 6, 1, 0), (SPREAD, 6, 1, 1), (ARRIVE, 3, 1, 0), (MULTIPLY, 2, 1, 0), (FORWARD, 2, 0, 0),
+    (HAND_OVER, 7, 1, 0), (FORWARD, 2, 0, 1), (ARRIVE, 3, 1, 1), (HAND_OVER, 1, 1, 0), (FORWARD, 6, 1, 0),
+    (FORWARD, 6, 1, 1), (ARRIVE, 3, 0, 0), (SPREAD, 5, 0, 0), (MULTIPLY, 2, 0, 0), (ARRIVE, 3, 0, 1),
+    (ARRIVE, 4, 1, 0), (SPREAD, 5, 0, 1), (SPREAD, 4, 1, 0), (MULTIPLY, 6, 1, 0), (FORWARD, 5, 0, 0),
+    (ARRIVE, 4, 0, 0), (HAND_OVER, 2, 1, 0), (FORWARD, 5, 0, 1), (ARRIVE, 4, 1, 1), (SPREAD, 4, 1, 1),
+    (SPREAD, 3, 0, 0), (SPREAD, 3, 0, 1), (FORWARD, 4, 1, 0), (HAND_OVER, 6, 1, 0), (SPREAD, 5, 1, 0),
+    (MULTIPLY, 5, 0, 0), (FORWARD, 4, 1, 1), (SPREAD, 5, 1, 1), (SPREAD, 4, 0, 0), (FORWARD, 3, 0, 0),
+    (FORWARD, 3, 0, 1), (MULTIPLY, 4, 1, 0), (ARRIVE, 4, 0, 1), (FORWARD, 5, 1, 0), (FORWARD, 5, 1, 1),
+    (SPREAD, 4, 0, 1), (SPREAD, 6, 0, 0), (FORWARD, 4, 0, 0), (SPREAD, 6, 0, 1), (MULTIPLY, 3, 0, 0),
+    (SPREAD, 3, 1, 0), (MULTIPLY, 5, 1, 0), (FORWARD, 4, 0, 1), (SPREAD, 3, 1, 1), (FORWARD, 6, 0, 0),
+    (HAND_OVER, 4, 1, 0), (SPREAD, 7, 0, 0), (SPREAD, 7, 0, 1), (FORWARD, 6, 0, 1), (MULTIPLY, 4, 0, 0),
+    (FORWARD, 3, 1, 0), (FORWARD, 3, 1, 1), (HAND_OVER, 5, 1, 0), (SPREAD, 1, 0, 0), (SPREAD, 1, 0, 1),
+    (FORWARD, 7, 0, 0), (MULTIPLY, 6, 0, 0), (FORWARD, 7, 0, 1), (MULTIPLY, 3, 1, 0), (FORWARD, 1, 0, 0),
+    (FORWARD, 1, 0, 1), (MULTIPLY, 7, 0, 0), (MULTIPLY, 1, 0, 0), (HAND_OVER, 3, 1, 0),
+)
 
 
 def kernel(ring, side, x_hbm, gain_hbm, wq_hbm, wk_hbm, wv_hbm, q_out, kv_out,
@@ -132,13 +155,12 @@
         reference = part(block, HALVES * quarter + half)[kind]
         remote(reference, reference, z_send.at[0], z_recv.at[(back * HALVES + half) * 2 + kind], at_ring(1)).wait_recv()
 
-    def ring_service(hop, half):
-        for kind in range(2):
-            for direction in range(2):
-                if hop <= reach(direction, half):
-                    ring_arrival(direction, hop, half, kind)
-                    if hop < reach(direction, half):
-                        ring_send(direction, hop, half, kind)
+    def ring_service(hop, kind, half):
+        for direction in range(2):
+            if hop <= reach(direction, half):
+                ring_arrival(direction, hop, half, kind)
+                if hop < reach(direction, half):
+                    ring_send(direction, hop, half, kind)
 
     def square_copy(r, lane_index, chunk, kind, device):
         block = (z + ring - r) % ring
@@ -146,27 +168,24 @@
         index = (r * 6 + lane_index) * 2 + kind
         return remote(reference, reference, xy_send.at[index], xy_recv.at[index], device)
 
-    def square_send(r, half):
-        for kind in range(2):
-            for base, device in ((0, x_peer), (2, y_peer)):
-                copy = square_copy(r, base + half, HALVES * quarter + half, kind, device)
-                copy.start()
-                started.append(copy)
-
-    def square_forward(r, half):
-        base, chunk, device = ((0, HALVES * quarter_x, y_peer), (2, HALVES * quarter_y, x_peer))[half]
-        for kind in range(2):
-            square_copy(r, base + half, chunk + half, kind, device).wait_recv()
-            copy = square_copy(r, 4 + half, chunk + half, kind, device)
+    def square_send(r, kind, half):
+        for base, device in ((0, x_peer), (2, y_peer)):
+            copy = square_copy(r, base + half, HALVES * quarter + half, kind, device)
             copy.start()
             started.append(copy)
 
-    def square_rest(r):
-        for kind in range(2):
-            square_copy(r, 1, HALVES * quarter_x + 1, kind, x_peer).wait_recv()
-            square_copy(r, 2, HALVES * quarter_y, kind, y_peer).wait_recv()
-            square_copy(r, 4, HALVES * quarter_d, kind, y_peer).wait_recv()
-            square_copy(r, 5, HALVES * quarter_d + 1, kind, x_peer).wait_recv()
+    def square_forward(r, kind, half):
+        base, chunk, device = ((0, HALVES * quarter_x, y_peer), (2, HALVES * quarter_y, x_peer))[half]
+        square_copy(r, base + half, chunk + half, kind, device).wait_recv()
+        copy = square_copy(r, 4 + half, chunk + half, kind, device)
+        copy.start()
+        started.append(copy)
+
+    def square_rest(r, kind):
+        square_copy(r, 1, HALVES * quarter_x + 1, kind, x_peer).wait_recv()
+        square_copy(r, 2, HALVES * quarter_y, kind, y_peer).wait_recv()
+        square_copy(r, 4, HALVES * quarter_d, kind, y_peer).wait_recv()
+        square_copy(r, 5, HALVES * quarter_d + 1, kind, x_peer).wait_recv()
 
     def flatten(block):
         @pl.loop(0, CHUNKS)
@@ -174,42 +193,42 @@
             span = pl.ds(pl.multiple_of(i * step, step), step)
             wflat[span, :] = wq[block, span].reshape(step, wflat.shape[1])
 
-    def product(block, slot, first):
+    def product(block, slot, kind, first):
         span = pl.ds(first, TILE)
-        q = jnp.dot(rows[span, :], wflat[...], preferred_element_type=jnp.float32)
-        oq[slot, span] = q.reshape((TILE,) + oq.shape[2:]).astype(oq.dtype)
-        kv = jnp.zeros((TILE, okv.shape[2]), jnp.float32)
-        for i in range(CHUNKS):
-            kv += lax.dot_general(rows[span, pl.ds(i * step, step)], wkv[block, i], (((1,), (1,)), ((), ())), preferred_element_type=jnp.float32)
-        okv[slot, span] = kv.astype(okv.dtype)
+        if kind == 0:
+            q = jnp.dot(rows[span, :], wflat[...], preferred_element_type=jnp.float32)
+            oq[slot, span] = q.reshape((TILE,) + oq.shape[2:]).astype(oq.dtype)
+        else:
+            kv = jnp.zeros((TILE, okv.shape[2]), jnp.float32)
+            for i in range(CHUNKS):
+                kv += lax.dot_general(rows[span, pl.ds(i * step, step)], wkv[block, i], (((1,), (1,)), ((), ())), preferred_element_type=jnp.float32)
+            okv[slot, span] = kv.astype(okv.dtype)
 
     def out_rows(block, first, count):
         return pl.ds(pl.multiple_of(block * chip_rows + first, TILE), count)
 
-    def out_copies(r, first, count):
+    def out_copy(r, kind, first, count):
         span, target = pl.ds(first, count), out_rows(z, first, count)
-        return (
-            remote(oq.at[r, span], q_out.at[target], oq_send.at[r], oq_recv.at[r], at_ring(r)),
-            remote(okv.at[r, span], kv_out.at[c, target], okv_send.at[r], okv_recv.at[r], at_ring(r)),
-        )
-
-    def multiply(r):
+        if kind == 0:
+            return remote(oq.at[r, span], q_out.at[target], oq_send.at[r], oq_recv.at[r], at_ring(r))
+        return remote(okv.at[r, span], kv_out.at[c, target], okv_send.at[r], okv_recv.at[r], at_ring(r))
+
+    def multiply(r, kind):
         block = (z + ring - r) % ring
-        flatten(block)
+        if kind == 0:
+            flatten(block)
 
         @pl.loop(0, tiles)
         def _(t):
             first = pl.multiple_of(t * TILE, TILE)
-            product(block, r, first)
-            for copy in out_copies(r, first, TILE):
-                copy.start()
-
-    def keep_copies():
+            product(block, r, kind, first)
+            if r:
+                out_copy(r, kind, first, TILE).start()
+
+    def keep_copy(kind):
         target = out_rows(z, 0, chip_rows)
-        return (
-            pltpu.make_async_copy(oq.at[0], q_out.at[target], keep_sem.at[0]),
-            pltpu.make_async_copy(okv.at[0], kv_out.at[c, target], keep_sem.at[1]),
-        )
+        source, kept = ((oq.at[0], q_out.at[target]), (okv.at[0], kv_out.at[c, target]))[kind]
+        return pltpu.make_async_copy(source, kept, keep_sem.at[kind])
 
     def hand_over(r, source):
         target = out_rows((z + r) % ring, 0, chip_rows)
@@ -224,19 +243,23 @@
         remote(okv.at[r], kv_out.at[c, target], okv_send.at[r], okv_recv.at[r], at_ring(r)).wait_recv()
         hand_over(r, kv_out.at[c, target]).start()
 
-    w_loads[0].wait()
-    for half in range(HALVES):
-        for direction in range(2):
-            ring_send(direction, 0, half, 0)
     for i in range(CHUNKS):
         pair_load(wk_hbm, i).wait()
     for half in range(HALVES):
         pair_arrival(half).wait_recv()
         for direction in range(2):
             ring_send(direction, 0, half, 1)
-
+    w_loads[0].wait()
+    for half in range(HALVES):
+        for direction in range(2):
+            ring_send(direction, 0, half, 0)
     gain_load.wait()
-    for i in range(4):
+
+    def row_copy(i, core):
+        span = pl.ds(pl.multiple_of(core * own + i * lane, lane), lane)
+        return remote(rows.at[span], rows.at[span], x_send.at[i], x_recv.at[i], partner)
+
+    def norm(i):
         x_loads[i].wait()
 
         @pl.loop(0, lane // NORM_ROWS)
@@ -246,75 +269,59 @@
             mean_sq = jnp.mean(wide * wide, axis=-1, keepdims=True)
             rows[span, :] = (wide * lax.rsqrt(mean_sq + EPSILON) * gain[...]).astype(rows.dtype)
 
-        span = pl.ds(own_first + i * lane, lane)
-        remote(rows.at[span], rows.at[span], x_send.at[i], x_recv.at[i], partner).start()
-
-    ring_service(1, 0)
-    square_send(ORDER[0], 0)
-
-    for i in range(4):
-        span = pl.ds(pl.multiple_of((1 - c) * own + i * lane, lane), lane)
-        remote(rows.at[span], rows.at[span], x_send.at[i], x_recv.at[i], partner).wait_recv()
-    for load in w_loads[1:]:
-        load.wait()
-    for i in range(HALVES, CHUNKS):
-        pair_arrival(i).wait_recv()
-    flatten(z)
-
-    def own_products(first_tile, count):
-        @pl.loop(first_tile, first_tile + count)
-        def _(t):
-            product(z, 0, pl.multiple_of(t * TILE, TILE))
-
-    own_products(0, tiles // 2)
-    ring_service(1, 1)
-    square_send(ORDER[0], 1)
-    own_products(tiles // 2, tiles - tiles // 2)
-    for copy in keep_copies():
-        copy.start()
-    hand_over(0, okv.at[0]).start()
-    square_forward(ORDER[0], 0)
-    ring_service(2, 0)
-    square_send(ORDER[1], 0)
-
-    services = {(0, 0): ((2, 1),), (0, 1): ((3, 0),), (1, 0): ((3, 1),), (1, 1): ((4, 0),), (2, 0): ((4, 1),)}
-    blocks = len(ORDER)
-    for j in range(blocks):
-        square_forward(ORDER[j], 1)
-        for hop, half in services.get((j, 0), ()):
-            ring_service(hop, half)
-        if j + 1 < blocks:
-            square_send(ORDER[j + 1], 1)
-            square_forward(ORDER[j + 1], 0)
-        for hop, half in services.get((j, 1), ()):
-            ring_service(hop, half)
-        if j + 2 < blocks:
-            square_send(ORDER[j + 2], 0)
-        square_rest(ORDER[j])
-        multiply(ORDER[j])
-        if j >= 3:
-            relay(ORDER[j - 3])
-
-    for r in ORDER[blocks - 3:]:
-        relay(r)
-    for r in ORDER:
+        row_copy(i, c).start()
+
+    normed = 0
+    rows_complete = False
+    for action, r, kind, half in SCHEDULE:
+        if action in (MULTIPLY, OWN) and not rows_complete:
+            rows_complete = True
+            for i in range(4):
+                row_copy(i, 1 - c).wait_recv()
+        if action == ARRIVE:
+            ring_service(r, kind, half)
+        elif action == SPREAD:
+            square_send(r, kind, half)
+        elif action == FORWARD:
+            square_forward(r, kind, half)
+        elif action == MULTIPLY:
+            square_rest(r, kind)
+            multiply(r, kind)
+        elif action == HAND_OVER:
+            relay(r)
+        elif action == NORM:
+            norm(normed)
+            normed += 1
+        elif kind == 0:
+            for load in w_loads[1:]:
+                load.wait()
+            multiply(0, 0)
+            keep_copy(0).start()
+        else:
+            for i in range(HALVES, CHUNKS):
+                pair_arrival(i).wait_recv()
+            multiply(0, 1)
+            keep_copy(1).start()
+            hand_over(0, okv.at[0]).start()
+
+    others = range(1, ring)
+    for r in others:
         target = out_rows((z + r) % ring, 0, chip_rows)
         remote(oq.at[r], q_out.at[target], oq_send.at[r], oq_recv.at[r], at_ring(r)).wait_recv()
     for r in range(ring):
         hand_arrival(r).wait_recv()
 
-    for copy in keep_copies():
-        copy.wait()
+    for kind in range(2):
+        keep_copy(kind).wait()
     for copy in started:
         copy.wait_send()
-    for r in ORDER:
-        for copy in out_copies(r, 0, chip_rows):
-            copy.wait_send()
+    for r in others:
+        for kind in range(2):
+            out_copy(r, kind, 0, chip_rows).wait_send()
     for r in range(ring):
         hand_over(r, okv.at[0]).wait_send()
     for i in range(4):
-        span = pl.ds(own_first + i * lane, lane)
-        remote(rows.at[span], rows.at[span], x_send.at[i], x_recv.at[i], partner).wait_send()
+        row_copy(i, c).wait_send()
     for i in range(CHUNKS):
         pair_copy(wk_hbm, i).wait_send()
 

time: 254 us -> 227 us (0.89)
  Pallas kernels: 244 us -> 219 us
    pallas_call x1, Pallas kernels: 244 us -> 219 us  [local_step(): pl.pallas_call(functools.partial(kernel, ring, side), out_shape=(jax.Shap...]
where the time goes in v2:
time: 227 us
  Pallas kernels  219 us (96%)
  local copies, waits for them, and re-layouts  6.67 us (3%)
    pallas_call x1, Pallas kernels, local_step(): pl.pallas_call(functools.partial(kernel, ring, side), out_shape=(jax.Shap...  219 us
    another operation x1, local copies, waits for them, and re-layouts, local_step(): return (q_out, kv_out[0][:, None, :], kv_out[1][:, None, :])  4.65 us

profile of v2, /device:TPU:22, one launch (start us, length us, event | category | flops | bytes accessed | tf_op | source)
XLA Modules:
  0.0 226.8 jit_solution(6577319649038090644)
XLA Ops:
  0.6 219.5 %shard_map.76 = (bf16[8192,2,128]{2,1,0:T(2,128)(2,1)}, bf16[2,8192,128]{2,1,0:T(8,128)(2,1)}) custom-call(bf16[512,4096]{1,0:T(8,128)(2,1)} %x_hbm.1, f32[1,4096]{1,0:T(1,128)} %bitcast.9, bf16[4096,2,128]{2,1,0:T(2,128)(2,1)} %wq_hbm.1, bf16[64,4096]{1,0:T(8,128)(2,1)} %bitcast.7, bf16[64,4096]{1,0:T(8,128)(2,1)} %bitcast.8), custom_call_target="tpu_custom_call" | custom-call | tf_op jit(solution)/shard_map/pallas_call | solution.py:342
  220.1 0.0 copy-start
  220.1 4.7 %slice_bitcast_fusion = (bf16[8192,1,128]{2,0,1:T(8,128)(2,1)}, bf16[8192,1,128]{2,0,1:T(8,128)(2,1)}) fusion(bf16[2,8192,128]{2,1,0:T(8,128)(2,1)} %get-tuple-element.6), kind=kLoop, calls=%fused_computation | loop fusion | bytes 8388608 | tf_op jit(solution)/shard_map/broadcast_in_dim;squeeze | solution.py:369
  224.8 0.0 copy-done
  224.8 2.0 copy.9
Async XLA Ops:
  220.1 4.7 %copy-start = (bf16[8192,2,128]{2,1,0:T(2,128)(2,1)S(1)}, bf16[8192,2,128]{2,1,0:T(2,128)(2,1)}, u32[]{:S(2)}) copy-start(bf16[8192,2,128]{2,1,0:T(2,128)(2,1)} %get-tuple-element.12) | copy-start | bytes 12582916

commit v3 on v2

v3 whole, which is shorter than its diff:
```python
import functools
import math

import jax
import jax.numpy as jnp
from jax import lax
from jax.experimental import pallas as pl
from jax.experimental.pallas import tpu as pltpu
from jax.sharding import PartitionSpec as P

EPSILON = 1e-6
MESH = pl.DeviceIdType.MESH
CORES = 2
QUARTERS = 4
HALVES = 2
CHUNKS = QUARTERS * HALVES
TILE = 256
NORM_ROWS = 16

PAIRS, PRODUCTS, ROWS, HANDED = 2, 3, 5, 6

ARRIVE, SPREAD, FORWARD, MULTIPLY, HAND_OVER, NORM, OWN = range(7)
SCHEDULE = (
    (NORM, 0, 0, 0), (NORM, 0, 0, 0), (NORM, 0, 0, 0), (ARRIVE, 1, 1, 0), (SPREAD, 7, 1, 0),
    (NORM, 0, 0, 0), (ARRIVE, 1, 1, 1), (SPREAD, 7, 1, 1), (SPREAD, 1, 1, 0), (SPREAD, 1, 1, 1),
    (OWN, 0, 1, 0), (OWN, 0, 0, 0), (ARRIVE, 1, 0, 0), (FORWARD, 7, 1, 0), (FORWARD, 7, 1, 1),
    (FORWARD, 1, 1, 0), (ARRIVE, 1, 0, 1), (FORWARD, 1, 1, 1), (ARRIVE, 2, 1, 0), (SPREAD, 2, 1, 0),
    (MULTIPLY, 7, 1, 0), (ARRIVE, 2, 1, 1), (SPREAD, 2, 1, 1), (MULTIPLY, 1, 1, 0), (FORWARD, 2, 1, 0),
    (ARRIVE, 2, 0, 0), (SPREAD, 6, 0, 0), (FORWARD, 2, 1, 1), (ARRIVE, 2, 0, 1), (SPREAD, 6, 0, 1),
    (ARRIVE, 3, 1, 0), (SPREAD, 5, 1, 0), (FORWARD, 6, 0, 0), (MULTIPLY, 2, 1, 0), (HAND_OVER, 7, 1, 0),
    (FORWARD, 6, 0, 1), (ARRIVE, 3, 1, 1), (SPREAD, 5, 1, 1), (HAND_OVER, 1, 1, 0), (FORWARD, 5, 1, 0),
    (ARRIVE, 3, 0, 0), (SPREAD, 3, 0, 0), (MULTIPLY, 6, 0, 0), (ARRIVE, 3, 0, 1), (FORWARD, 5, 1, 1),
    (SPREAD, 3, 0, 1), (ARRIVE, 4, 1, 0), (SPREAD, 4, 1, 0), (FORWARD, 3, 0, 0), (MULTIPLY, 5, 1, 0),
    (ARRIVE, 4, 0, 0), (HAND_OVER, 2, 1, 0), (FORWARD, 3, 0, 1), (ARRIVE, 4, 1, 1), (SPREAD, 4, 1, 1),
    (SPREAD, 5, 0, 0), (SPREAD, 5, 0, 1), (FORWARD, 4, 1, 0), (ARRIVE, 4, 0, 1), (SPREAD, 3, 1, 0),
    (MULTIPLY, 3, 0, 0), (FORWARD, 4, 1, 1), (SPREAD, 3, 1, 1), (SPREAD, 4, 0, 0), (FORWARD, 5, 0, 0),
    (SPREAD, 4, 0, 1), (FORWARD, 5, 0, 1), (FORWARD, 3, 1, 0), (MULTIPLY, 4, 1, 0), (FORWARD, 3, 1, 1),
    (SPREAD, 2, 0, 0), (HAND_OVER, 5, 1, 0), (FORWARD, 4, 0, 0), (SPREAD, 2, 0, 1), (FORWARD, 4, 0, 1),
    (MULTIPLY, 5, 0, 0), (SPREAD, 6, 1, 0), (MULTIPLY, 3, 1, 0), (SPREAD, 6, 1, 1), (FORWARD, 2, 0, 0),
    (HAND_OVER, 4, 1, 0), (SPREAD, 1, 0, 0), (SPREAD, 1, 0, 1), (FORWARD, 2, 0, 1), (MULTIPLY, 4, 0, 0),
    (FORWARD, 6, 1, 0), (FORWARD, 6, 1, 1), (SPREAD, 7, 0, 0), (HAND_OVER, 3, 1, 0), (SPREAD, 7, 0, 1),
    (FORWARD, 1, 0, 0), (FORWARD, 1, 0, 1), (MULTIPLY, 2, 0, 0), (MULTIPLY, 6, 1, 0), (FORWARD, 7, 0, 0),
    (FORWARD, 7, 0, 1), (MULTIPLY, 1, 0, 0), (MULTIPLY, 7, 0, 0), (HAND_OVER, 6, 1, 0),
)


def kernel(ring, side, x_hbm, gain_hbm, wq_hbm, wk_hbm, wv_hbm, q_out, kv_out,
           rows, gain, wq, wkv, wflat, oq, okv,
           local_sem, send_sem, recv_sem, z_recv, xy_recv, okv_recv, keep_sem):
    dp, tp = lax.axis_index("dp"), lax.axis_index("tp")
    z, c = tp // CORES, tp % CORES
    grid_x, grid_y = dp // side, dp % side
    odd_x, odd_y = grid_x % 2, grid_y % 2
    quarter = 2 * odd_x + odd_y
    quarter_x, quarter_y, quarter_d = 2 * (1 - odd_x) + odd_y, 2 * odd_x + 1 - odd_y, 3 - quarter
    x_peer = (dp + side * (1 - 2 * odd_x), tp)
    y_peer = (dp + 1 - 2 * odd_y, tp)
    partner = (dp, tp + 1 - 2 * c)

    own, depth = x_hbm.shape
    chip_rows = CORES * own
    step = depth // CHUNKS
    piece = wk_hbm.shape[0]
    tiles = chip_rows // TILE

    def at_ring(distance):
        return (dp, CORES * ((z + ring - distance) % ring) + c)

    def remote(src, dst, send, recv, device):
        return pltpu.make_async_remote_copy(src_ref=src, dst_ref=dst, send_sem=send, recv_sem=recv, device_id=device, device_id_type=MESH)

    def part(block, chunk):
        first = pl.multiple_of(chunk * step, step)
        return wq.at[block, pl.ds(first, step)], wkv.at[block, chunk]

    own_first = pl.multiple_of(c * own, own)
    lane = own // 4
    x_loads = [pltpu.make_async_copy(x_hbm.at[pl.ds(i * lane, lane)], rows.at[pl.ds(own_first + i * lane, lane)], local_sem.at[i]) for i in range(4)]
    w_loads = []
    for i in range(QUARTERS):
        first = pl.multiple_of(((quarter + i) % QUARTERS) * (depth // QUARTERS), depth // QUARTERS)
        w_loads.append(pltpu.make_async_copy(wq_hbm.at[pl.ds(first, depth // QUARTERS)], wq.at[z, pl.ds(first, depth // QUARTERS)], local_sem.at[4 + min(i, 1)]))
    gain_load = pltpu.make_async_copy(gain_hbm, gain, local_sem.at[6])
    own_half = pl.ds(pl.multiple_of(c * piece, piece), piece)

    def columns(i):
        chunk = (HALVES * quarter + i) % CHUNKS
        return chunk, pl.ds(pl.multiple_of(chunk * step, step), step)

    def pair_load(source, i):
        chunk, span = columns(i)
        return pltpu.make_async_copy(source.at[:, span], wkv.at[z, chunk, own_half], local_sem.at[7])

    def pair_copy(source, i):
        chunk, span = columns(i)
        return remote(source.at[:, span], wkv.at[z, chunk, own_half], send_sem.at[PAIRS], recv_sem.at[3], partner)

    def pair_wait():
        pieces = wkv.at[z, :, own_half]
        remote(pieces, pieces, send_sem.at[PAIRS], recv_sem.at[3], partner).wait_recv()

    w_loads[0].start()
    for load in x_loads:
        load.start()
    gain_load.start()

    @pl.when(c == 0)
    def _():
        for i in range(CHUNKS):
            pair_load(wk_hbm, i).start()

    @pl.when(c == 1)
    def _():
        for i in range(CHUNKS):
            pair_load(wv_hbm, i).start()

    for load in w_loads[1:]:
        load.start()

    barrier = pltpu.get_barrier_semaphore()
    above, below = CORES * ((z + 1) % ring), CORES * ((z + ring - 1) % ring)
    peers = [x_peer, y_peer, partner] + [at_ring(r) for r in range(1, ring)] + [(dp, above + 1 - c), (dp, below + 1 - c)]
    for peer in peers:
        pl.semaphore_signal(barrier, inc=1, device_id=peer, device_id_type=MESH)
    pl.semaphore_wait(barrier, len(peers))

    def pair_start():
        @pl.when(c == 0)
        def _():
            for i in range(CHUNKS):
                pair_copy(wv_hbm, i).start()

        @pl.when(c == 1)
        def _():
            for i in range(CHUNKS):
                pair_copy(wk_hbm, i).start()

    half_ring = ring // 2

    def ring_send(direction, hop, half, kind):
        back = hop if direction == 0 else ring - hop
        block = (z + ring - back) % ring
        reference = part(block, HALVES * quarter + half)[kind]
        landed = (hop + 1) if direction == 0 else ring - hop - 1
        copy = remote(reference, reference, send_sem.at[kind], z_recv.at[(landed * HALVES + half) * 2 + kind], at_ring(ring - 1 if direction == 0 else 1))
        copy.start()

    def reach(direction, half):
        return half_ring if direction == half else half_ring - 1

    def key_value_start(half):
        chunk, span = columns(half)
        for direction in range(2):
            landed = 1 if direction == 0 else ring - 1
            for core, source in enumerate((wk_hbm, wv_hbm)):
                device = (dp, CORES * ((z + landed) % ring) + core)
                remote(source.at[:, span], wkv.at[z, chunk, own_half], send_sem.at[1], z_recv.at[(landed * HALVES + half) * 2 + 1], device).start()

    def ring_arrival(direction, hop, half, kind):
        back = hop if direction == 0 else ring - hop
        block = (z + ring - back) % ring
        reference = part(block, HALVES * quarter + half)[kind]
        remote(reference, reference, send_sem.at[kind], z_recv.at[(back * HALVES + half) * 2 + kind], at_ring(1)).wait_recv()

    def ring_service(hop, kind, half):
        for direction in range(2):
            if hop <= reach(direction, half):
                ring_arrival(direction, hop, half, kind)
                if hop < reach(direction, half):
                    ring_send(direction, hop, half, kind)

    def square_copy(r, lane_index, chunk, kind, device):
        block = (z + ring - r) % ring
        reference = part(block, chunk)[kind]
        index = (r * 3 + {0: 0, 3: 1}.get(lane_index, 2)) * 2 + kind
        return remote(reference, reference, send_sem.at[kind], xy_recv.at[index], device)

    def square_send(r, kind, half):
        for base, device in ((0, x_peer), (2, y_peer)):
            square_copy(r, base + half, HALVES * quarter + half, kind, device).start()

    def square_forward(r, kind, half):
        lane_index, chunk, device = ((0, HALVES * quarter_x, y_peer), (3, HALVES * quarter_y + 1, x_peer))[half]
        square_copy(r, lane_index, chunk, kind, device).wait_recv()
        square_copy(r, 4 + half, chunk, kind, device).start()

    def square_rest(r, kind):
        block = (z + ring - r) % ring
        four = (wq.at[block, pl.ds(0, 4 * step)], wkv.at[block, pl.ds(0, 4)])[kind]
        remote(four, four, send_sem.at[kind], xy_recv.at[(r * 3 + 2) * 2 + kind], x_peer).wait_recv()

    def flatten(block):
        @pl.loop(0, CHUNKS)
        def _(i):
            span = pl.ds(pl.multiple_of(i * step, step), step)
            wflat[span, :] = wq[block, span].reshape(step, wflat.shape[1])

    def product(block, slot, kind, first):
        span = pl.ds(first, TILE)
        if kind == 0:
            q = jnp.dot(rows[span, :], wflat[...], preferred_element_type=jnp.float32)
            oq[slot, span] = q.reshape((TILE,) + oq.shape[2:]).astype(oq.dtype)
        else:
            kv = jnp.zeros((TILE, okv.shape[2]), jnp.float32)
            for i in range(CHUNKS):
                kv += lax.dot_general(rows[span, pl.ds(i * step, step)], wkv[block, i], (((1,), (1,)), ((), ())), preferred_element_type=jnp.float32)
            okv[slot, span] = kv.astype(okv.dtype)

    def out_rows(block, first, count):
        return pl.ds(pl.multiple_of(block * chip_rows + first, TILE), count)

    def out_copy(r, kind, first, count):
        span, target = pl.ds(first, count), out_rows(z, first, count)
        if kind == 0:
            return remote(oq.at[r, span], q_out.at[target], send_sem.at[PRODUCTS], recv_sem.at[0], at_ring(r))
        return remote(okv.at[r, span], kv_out.at[c, target], send_sem.at[PRODUCTS + 1], okv_recv.at[r], at_ring(r))

    def multiply(r, kind):
        block = (z + ring - r) % ring
        if kind == 0:
            flatten(block)

        @pl.loop(0, tiles)
        def _(t):
            first = pl.multiple_of(t * TILE, TILE)
            product(block, r, kind, first)
            if r:
                out_copy(r, kind, first, TILE).start()

    def keep_copy(kind):
        target = out_rows(z, 0, chip_rows)
        source, kept = ((oq.at[0], q_out.at[target]), (okv.at[0], kv_out.at[c, target]))[kind]
        return pltpu.make_async_copy(source, kept, keep_sem.at[kind])

    def hand_over(r, source):
        target = out_rows((z + r) % ring, 0, chip_rows)
        return remote(source, kv_out.at[c, target], send_sem.at[HANDED], recv_sem.at[1], partner)

    def relay(r):
        target = out_rows((z + r) % ring, 0, chip_rows)
        remote(okv.at[r], kv_out.at[c, target], send_sem.at[PRODUCTS + 1], okv_recv.at[r], at_ring(r)).wait_recv()
        hand_over(r, kv_out.at[c, target]).start()

    for half in range(HALVES):
        key_value_start(half)
    w_loads[0].wait()
    for half in range(HALVES):
        for direction in range(2):
            ring_send(direction, 0, half, 0)
    pair_start()
    for i in range(CHUNKS):
        pair_load(wk_hbm, i).wait()
    gain_load.wait()

    def row_copy(i, core):
        span = pl.ds(pl.multiple_of(core * own + i * lane, lane), lane)
        return remote(rows.at[span], rows.at[span], send_sem.at[ROWS], recv_sem.at[2], partner)

    def half_rows(core):
        span = pl.ds(pl.multiple_of(core * own, own), own)
        return remote(rows.at[span], rows.at[span], send_sem.at[ROWS], recv_sem.at[2], partner)

    def norm(i):
        x_loads[i].wait()

        @pl.loop(0, lane // NORM_ROWS)
        def _(n):
            span = pl.ds(pl.multiple_of(own_first + i * lane + n * NORM_ROWS, NORM_ROWS), NORM_ROWS)
            wide = rows[span, :].astype(jnp.float32)
            mean_sq = jnp.mean(wide * wide, axis=-1, keepdims=True)
            rows[span, :] = (wide * lax.rsqrt(mean_sq + EPSILON) * gain[...]).astype(rows.dtype)

        row_copy(i, c).start()

    normed = 0
    rows_complete = False
    for action, r, kind, half in SCHEDULE:
        if action in (MULTIPLY, OWN) and not rows_complete:
            rows_complete = True
            half_rows(1 - c).wait_recv()
        if action == ARRIVE:
            ring_service(r, kind, half)
        elif action == SPREAD:
            square_send(r, kind, half)
        elif action == FORWARD:
            square_forward(r, kind, half)
        elif action == MULTIPLY:
            square_rest(r, kind)
            multiply(r, kind)
        elif action == HAND_OVER:
            relay(r)
        elif action == NORM:
            norm(normed)
            normed += 1
        elif kind == 0:
            for load in w_loads[1:]:
                load.wait()
            multiply(0, 0)
            keep_copy(0).start()
        else:
            pair_wait()
            multiply(0, 1)
            keep_copy(1).start()
            hand_over(0, okv.at[0]).start()

    for kind in range(2):
        keep_copy(kind).wait()

    def whole(source, target, send, recv):
        return remote(source, target, send_sem.at[send], recv_sem.at[recv], partner)

    others = ring - 1
    products = q_out.at[pl.ds(0, others * chip_rows)]
    whole(products, products, PRODUCTS, 0).wait_recv()
    heads = kv_out.at[1 - c]
    whole(heads, heads, HANDED, 1).wait()
    half_rows(c).wait_send()
    for kind, weights in enumerate((wq, wkv)):
        sent = weights.at[pl.ds(0, others)]
        whole(sent, sent, kind, 0).wait_send()
    for kind, buffer in enumerate((oq, okv)):
        sent = buffer.at[pl.ds(0, others)]
        whole(sent, sent, PRODUCTS + kind, 0).wait_send()
    pieces = wkv.at[z, :, own_half]
    whole(pieces, pieces, PAIRS, 0).wait_send()


def flush(q_ref, kv_ref, q_out, k_out, v_out, sem):
    copies = [pltpu.make_async_copy(source, target, sem.at[i]) for i, (source, target) in enumerate(((q_ref, q_out), (kv_ref.at[0], k_out), (kv_ref.at[1], v_out)))]
    for copy in copies:
        copy.start()
    for copy in copies:
        copy.wait()


def solution(mesh):
    ring = mesh.shape["tp"] // CORES
    side = math.isqrt(mesh.shape["dp"])
    assert side * side == mesh.shape["dp"] and side % 2 == 0

    def local_step(x_rows, norm_gain, w_q, w_k, w_v):
        own, depth = x_rows.shape
        heads, width = w_q.shape[1:]
        piece = w_k.shape[1]
        assert piece * CORES == width
        tokens, chip_rows, step = own * CORES * ring, own * CORES, depth // CHUNKS
        dma = pltpu.SemaphoreType.DMA
        bf16 = x_rows.dtype
        q_out, kv_out = pl.pallas_call(
            functools.partial(kernel, ring, side),
            out_shape=(
                jax.ShapeDtypeStruct((tokens, heads, width), bf16),
                jax.ShapeDtypeStruct((CORES, tokens, width), bf16),
            ),
            in_specs=[pl.BlockSpec(memory_space=pltpu.HBM)] * 5,
            out_specs=(pl.BlockSpec(memory_space=pl.ANY),) * 2,
            scratch_shapes=[
                pltpu.VMEM((chip_rows, depth), bf16),
                pltpu.VMEM((1, depth), jnp.float32),
                pltpu.VMEM((ring, depth, heads, width), bf16),
                pltpu.VMEM((ring, CHUNKS, width, step), bf16),
                pltpu.VMEM((depth, heads * width), bf16),
                pltpu.VMEM((ring, chip_rows, heads, width), bf16),
                pltpu.VMEM((ring, chip_rows, width), bf16),
                dma((8,)), dma((HANDED + 1,)), dma((4,)),
                dma((ring * HALVES * 2,)), dma((ring * 3 * 2,)), dma((ring,)), dma((2,)),
            ],
            compiler_params=pltpu.CompilerParams(collective_id=0, has_side_effects=True, vmem_limit_bytes=42 * 1024 * 1024),
        )(*(pltpu.with_memory_space_constraint(a, pltpu.HBM) for a in (x_rows, norm_gain.reshape(1, depth), w_q, w_k.T, w_v.T)))
        head = jax.ShapeDtypeStruct((tokens, width), bf16)
        q_out, k_out, v_out = pl.pallas_call(
            flush,
            out_shape=(jax.ShapeDtypeStruct((tokens, heads, width), bf16), head, head),
            in_specs=[pl.BlockSpec(memory_space=pl.ANY)] * 2,
            out_specs=(pl.BlockSpec(memory_space=pl.ANY),) * 3,
            scratch_shapes=[dma((3,))],
            compiler_params=pltpu.CompilerParams(vmem_limit_bytes=1024 * 1024),
        )(q_out, kv_out)
        return q_out, k_out[:, None, :], v_out[:, None, :]

    return jax.shard_map(local_step, mesh=mesh, in_specs=(P(("dp", "tp"), None), P(None), P(None, "tp", None), P(None, "tp"), P(None, "tp")), out_specs=(P("dp", "tp", None), P("dp", "tp", None), P("dp", "tp", None)), check_vma=False)
```

time: 227 us -> 216 us (0.952)
  local copies, waits for them, and re-layouts: 6.67 us -> 0 us
  Pallas kernels: 219 us -> 215 us
    pallas_call x1, Pallas kernels: 219 us -> 212 us  [local_step(): pl.pallas_call(functools.partial(kernel, ring, side), out_shape=(jax.Shap...]
    another operation x1 -> x0, local copies, waits for them, and re-layouts: 4.65 us -> none  [local_step(): return (q_out, kv_out[0][:, None, :], kv_out[1][:, None, :])]
    pallas_call x0 -> x1, Pallas kernels: none -> 3.36 us  [local_step(): pl.pallas_call(flush, out_shape=(jax.ShapeDtypeStruct((tokens, heads, wid...]
where the time goes in v3:
time: 216 us
  Pallas kernels  215 us (100%)
    pallas_call x1, Pallas kernels, local_step(): pl.pallas_call(functools.partial(kernel, ring, side), out_shape=(jax.Shap...  212 us

profile of v3, /device:TPU:22, one launch (start us, length us, event | category | flops | bytes accessed | tf_op | source)
XLA Modules:
  0.0 215.9 jit_solution(18397075086456441319)
XLA Ops:
  0.6 211.9 %shard_map.76 = (bf16[8192,2,128]{2,1,0:T(2,128)(2,1)S(1)}, bf16[2,8192,128]{2,1,0:T(8,128)(2,1)S(1)}) custom-call(bf16[512,4096]{1,0:T(8,128)(2,1)} %x_hbm.1, f32[1,4096]{1,0:T(1,128)} %bitcast.7, bf16[4096,2,128]{2,1,0:T(2,128)(2,1)} %wq_hbm.1, bf16[64,4096]{1,0:T(8,128)(2,1)} %bitcast.5, bf16[64,4096]{1,0:T(8,128)(2,1)} %bitcast.6), custom_call_target="tpu_custom_call" | custom-call | tf_op jit(solution)/shard_map/pallas_call | solution.py:349
  212.5 3.4 %shard_map.77 = (bf16[8192,2,128]{2,1,0:T(2,128)(2,1)}, bf16[8192,128]{1,0:T(8,128)(2,1)}, bf16[8192,128]{1,0:T(8,128)(2,1)}) custom-call(bf16[8192,2,128]{2,1,0:T(2,128)(2,1)S(1)} %get-tuple-element.8.q_ref, bf16[2,8192,128]{2,1,0:T(8,128)(2,1)S(1)} %get-tuple-element.9.kv_ref), custom_call_target="tpu_custom_call" | custom-call | tf_op jit(solution)/shard_map/pallas_call | solution.py:371

commit v4 on v3

--- a/solution.py
+++ b/solution.py
@@ -14,33 +14,33 @@
 QUARTERS = 4
 HALVES = 2
 CHUNKS = QUARTERS * HALVES
-TILE = 256
+TILE = 128
 NORM_ROWS = 16
 
 PAIRS, PRODUCTS, ROWS, HANDED = 2, 3, 5, 6
 
 ARRIVE, SPREAD, FORWARD, MULTIPLY, HAND_OVER, NORM, OWN = range(7)
 SCHEDULE = (
-    (NORM, 0, 0, 0), (NORM, 0, 0, 0), (NORM, 0, 0, 0), (ARRIVE, 1, 1, 0), (SPREAD, 7, 1, 0),
-    (NORM, 0, 0, 0), (ARRIVE, 1, 1, 1), (SPREAD, 7, 1, 1), (SPREAD, 1, 1, 0), (SPREAD, 1, 1, 1),
-    (OWN, 0, 1, 0), (OWN, 0, 0, 0), (ARRIVE, 1, 0, 0), (FORWARD, 7, 1, 0), (FORWARD, 7, 1, 1),
-    (FORWARD, 1, 1, 0), (ARRIVE, 1, 0, 1), (FORWARD, 1, 1, 1), (ARRIVE, 2, 1, 0), (SPREAD, 2, 1, 0),
-    (MULTIPLY, 7, 1, 0), (ARRIVE, 2, 1, 1), (SPREAD, 2, 1, 1), (MULTIPLY, 1, 1, 0), (FORWARD, 2, 1, 0),
-    (ARRIVE, 2, 0, 0), (SPREAD, 6, 0, 0), (FORWARD, 2, 1, 1), (ARRIVE, 2, 0, 1), (SPREAD, 6, 0, 1),
-    (ARRIVE, 3, 1, 0), (SPREAD, 5, 1, 0), (FORWARD, 6, 0, 0), (MULTIPLY, 2, 1, 0), (HAND_OVER, 7, 1, 0),
-    (FORWARD, 6, 0, 1), (ARRIVE, 3, 1, 1), (SPREAD, 5, 1, 1), (HAND_OVER, 1, 1, 0), (FORWARD, 5, 1, 0),
-    (ARRIVE, 3, 0, 0), (SPREAD, 3, 0, 0), (MULTIPLY, 6, 0, 0), (ARRIVE, 3, 0, 1), (FORWARD, 5, 1, 1),
-    (SPREAD, 3, 0, 1), (ARRIVE, 4, 1, 0), (SPREAD, 4, 1, 0), (FORWARD, 3, 0, 0), (MULTIPLY, 5, 1, 0),
-    (ARRIVE, 4, 0, 0), (HAND_OVER, 2, 1, 0), (FORWARD, 3, 0, 1), (ARRIVE, 4, 1, 1), (SPREAD, 4, 1, 1),
-    (SPREAD, 5, 0, 0), (SPREAD, 5, 0, 1), (FORWARD, 4, 1, 0), (ARRIVE, 4, 0, 1), (SPREAD, 3, 1, 0),
-    (MULTIPLY, 3, 0, 0), (FORWARD, 4, 1, 1), (SPREAD, 3, 1, 1), (SPREAD, 4, 0, 0), (FORWARD, 5, 0, 0),
-    (SPREAD, 4, 0, 1), (FORWARD, 5, 0, 1), (FORWARD, 3, 1, 0), (MULTIPLY, 4, 1, 0), (FORWARD, 3, 1, 1),
-    (SPREAD, 2, 0, 0), (HAND_OVER, 5, 1, 0), (FORWARD, 4, 0, 0), (SPREAD, 2, 0, 1), (FORWARD, 4, 0, 1),
-    (MULTIPLY, 5, 0, 0), (SPREAD, 6, 1, 0), (MULTIPLY, 3, 1, 0), (SPREAD, 6, 1, 1), (FORWARD, 2, 0, 0),
-    (HAND_OVER, 4, 1, 0), (SPREAD, 1, 0, 0), (SPREAD, 1, 0, 1), (FORWARD, 2, 0, 1), (MULTIPLY, 4, 0, 0),
-    (FORWARD, 6, 1, 0), (FORWARD, 6, 1, 1), (SPREAD, 7, 0, 0), (HAND_OVER, 3, 1, 0), (SPREAD, 7, 0, 1),
-    (FORWARD, 1, 0, 0), (FORWARD, 1, 0, 1), (MULTIPLY, 2, 0, 0), (MULTIPLY, 6, 1, 0), (FORWARD, 7, 0, 0),
-    (FORWARD, 7, 0, 1), (MULTIPLY, 1, 0, 0), (MULTIPLY, 7, 0, 0), (HAND_OVER, 6, 1, 0),
+    (ARRIVE, 1, 1, 0), (SPREAD, 7, 1, 0), (NORM, 0, 0, 0), (ARRIVE, 1, 1, 1), (SPREAD, 1, 1, 1),
+    (SPREAD, 7, 1, 1), (SPREAD, 1, 1, 0), (NORM, 0, 0, 0), (FORWARD, 1, 1, 1), (FORWARD, 7, 1, 0),
+    (FORWARD, 7, 1, 1), (ARRIVE, 1, 0, 0), (ARRIVE, 1, 0, 1), (FORWARD, 1, 1, 0), (ARRIVE, 2, 1, 0),
+    (SPREAD, 6, 1, 0), (ARRIVE, 2, 1, 1), (SPREAD, 2, 1, 0), (SPREAD, 2, 1, 1), (ARRIVE, 2, 0, 0),
+    (SPREAD, 6, 0, 0), (ARRIVE, 2, 0, 1), (SPREAD, 6, 0, 1), (NORM, 0, 0, 0), (NORM, 0, 0, 0),
+    (FORWARD, 6, 0, 0), (FORWARD, 2, 1, 0), (ARRIVE, 3, 1, 1), (SPREAD, 3, 1, 1), (ARRIVE, 3, 1, 0),
+    (FORWARD, 2, 1, 1), (FORWARD, 6, 0, 1), (ARRIVE, 3, 0, 0), (ARRIVE, 3, 0, 1), (SPREAD, 3, 0, 1),
+    (SPREAD, 3, 0, 0), (SPREAD, 5, 1, 1), (SPREAD, 5, 1, 0), (MULTIPLY, 1, 1, 0), (MULTIPLY, 6, 0, 0),
+    (ARRIVE, 4, 0, 1), (MULTIPLY, 2, 1, 0), (FORWARD, 3, 0, 0), (FORWARD, 3, 0, 1), (FORWARD, 5, 1, 1),
+    (MULTIPLY, 7, 1, 0), (FORWARD, 5, 1, 0), (ARRIVE, 4, 1, 0), (SPREAD, 5, 0, 0), (ARRIVE, 4, 1, 1),
+    (OWN, 0, 1, 0), (MULTIPLY, 3, 0, 0), (SPREAD, 4, 1, 0), (SPREAD, 5, 0, 1), (ARRIVE, 4, 0, 0),
+    (SPREAD, 4, 1, 1), (MULTIPLY, 5, 1, 0), (SPREAD, 3, 1, 0), (FORWARD, 4, 1, 0), (SPREAD, 6, 1, 1),
+    (FORWARD, 5, 0, 0), (FORWARD, 4, 1, 1), (FORWARD, 5, 0, 1), (FORWARD, 6, 1, 0), (FORWARD, 6, 1, 1),
+    (MULTIPLY, 4, 1, 0), (SPREAD, 4, 0, 1), (HAND_OVER, 1, 1, 0), (FORWARD, 3, 1, 0), (FORWARD, 3, 1, 1),
+    (MULTIPLY, 6, 1, 0), (SPREAD, 4, 0, 0), (FORWARD, 4, 0, 1), (SPREAD, 2, 0, 1), (MULTIPLY, 3, 1, 0),
+    (MULTIPLY, 5, 0, 0), (FORWARD, 4, 0, 0), (SPREAD, 2, 0, 0), (HAND_OVER, 7, 1, 0), (SPREAD, 1, 0, 0),
+    (MULTIPLY, 4, 0, 0), (HAND_OVER, 3, 1, 0), (FORWARD, 2, 0, 0), (FORWARD, 2, 0, 1), (SPREAD, 1, 0, 1),
+    (SPREAD, 7, 0, 1), (OWN, 0, 0, 0), (SPREAD, 7, 0, 0), (MULTIPLY, 2, 0, 0), (FORWARD, 1, 0, 0),
+    (HAND_OVER, 2, 1, 0), (FORWARD, 1, 0, 1), (FORWARD, 7, 0, 0), (FORWARD, 7, 0, 1), (HAND_OVER, 5, 1, 0),
+    (HAND_OVER, 4, 1, 0), (MULTIPLY, 1, 0, 0), (MULTIPLY, 7, 0, 0), (HAND_OVER, 6, 1, 0),
 )
 
 
@@ -73,6 +73,12 @@
         first = pl.multiple_of(chunk * step, step)
         return wq.at[block, pl.ds(first, step)], wkv.at[block, chunk]
 
+    barrier = pltpu.get_barrier_semaphore()
+    above, below = CORES * ((z + 1) % ring), CORES * ((z + ring - 1) % ring)
+    peers = [x_peer, y_peer, partner] + [at_ring(1), at_ring(ring - 1)] + [(dp, above + 1 - c), (dp, below + 1 - c)]
+    for peer in peers:
+        pl.semaphore_signal(barrier, inc=1, device_id=peer, device_id_type=MESH)
+
     own_first = pl.multiple_of(c * own, own)
     lane = own // 4
     x_loads = [pltpu.make_async_copy(x_hbm.at[pl.ds(i * lane, lane)], rows.at[pl.ds(own_first + i * lane, lane)], local_sem.at[i]) for i in range(4)]
@@ -117,11 +123,6 @@
     for load in w_loads[1:]:
         load.start()
 
-    barrier = pltpu.get_barrier_semaphore()
-    above, below = CORES * ((z + 1) % ring), CORES * ((z + ring - 1) % ring)
-    peers = [x_peer, y_peer, partner] + [at_ring(r) for r in range(1, ring)] + [(dp, above + 1 - c), (dp, below + 1 - c)]
-    for peer in peers:
-        pl.semaphore_signal(barrier, inc=1, device_id=peer, device_id_type=MESH)
     pl.semaphore_wait(barrier, len(peers))
 
     def pair_start():
@@ -155,6 +156,12 @@
             for core, source in enumerate((wk_hbm, wv_hbm)):
                 device = (dp, CORES * ((z + landed) % ring) + core)
                 remote(source.at[:, span], wkv.at[z, chunk, own_half], send_sem.at[1], z_recv.at[(landed * HALVES + half) * 2 + 1], device).start()
+
+    def query_start(half):
+        span = pl.ds(pl.multiple_of((HALVES * quarter + half) * step, step), step)
+        for direction in range(2):
+            landed = 1 if direction == 0 else ring - 1
+            remote(wq_hbm.at[span], wq.at[z, span], send_sem.at[0], z_recv.at[(landed * HALVES + half) * 2], at_ring(ring - landed)).start()
 
     def ring_arrival(direction, hop, half, kind):
         back = hop if direction == 0 else ring - hop
@@ -243,10 +250,8 @@
 
     for half in range(HALVES):
         key_value_start(half)
-    w_loads[0].wait()
     for half in range(HALVES):
-        for direction in range(2):
-            ring_send(direction, 0, half, 0)
+        query_start(half)
     pair_start()
     for i in range(CHUNKS):
         pair_load(wk_hbm, i).wait()
@@ -293,7 +298,7 @@
             norm(normed)
             normed += 1
         elif kind == 0:
-            for load in w_loads[1:]:
+            for load in w_loads:
                 load.wait()
             multiply(0, 0)
             keep_copy(0).start()

time: 216 us -> 214 us (level)
  Pallas kernels: 215 us -> 211 us
    pallas_call x1, Pallas kernels: 212 us -> 208 us  [local_step(): pl.pallas_call(functools.partial(kernel, ring, side), out_shape=(jax.Shap...]
where the time goes in v4:
time: 214 us; the launch traced here: 212 us
  Pallas kernels  211 us (99%)
    pallas_call x1, Pallas kernels, local_step(): pl.pallas_call(functools.partial(kernel, ring, side), out_shape=(jax.Shap...  208 us

profile of v4, /device:TPU:22, one launch (start us, length us, event | category | flops | bytes accessed | tf_op | source)
XLA Modules:
  0.0 212.0 jit_solution(335142651857479904)
XLA Ops:
  0.6 208.0 %shard_map.76 = (bf16[8192,2,128]{2,1,0:T(2,128)(2,1)S(1)}, bf16[2,8192,128]{2,1,0:T(8,128)(2,1)S(1)}) custom-call(bf16[512,4096]{1,0:T(8,128)(2,1)} %x_hbm.1, f32[1,4096]{1,0:T(1,128)} %bitcast.7, bf16[4096,2,128]{2,1,0:T(2,128)(2,1)} %wq_hbm.1, bf16[64,4096]{1,0:T(8,128)(2,1)} %bitcast.5, bf16[64,4096]{1,0:T(8,128)(2,1)} %bitcast.6), custom_call_target="tpu_custom_call" | custom-call | tf_op jit(solution)/shard_map/pallas_call | solution.py:354
  208.7 3.4 %shard_map.77 = (bf16[8192,2,128]{2,1,0:T(2,128)(2,1)}, bf16[8192,128]{1,0:T(8,128)(2,1)}, bf16[8192,128]{1,0:T(8,128)(2,1)}) custom-call(bf16[8192,2,128]{2,1,0:T(2,128)(2,1)S(1)} %get-tuple-element.8.q_ref, bf16[2,8192,128]{2,1,0:T(8,128)(2,1)S(1)} %get-tuple-element.9.kv_ref), custom_call_target="tpu_custom_call" | custom-call | tf_op jit(solution)/shard_map/pallas_call | solution.py:376

commit v5 on v4

--- a/solution.py
+++ b/solution.py
@@ -21,26 +21,26 @@
 
 ARRIVE, SPREAD, FORWARD, MULTIPLY, HAND_OVER, NORM, OWN = range(7)
 SCHEDULE = (
-    (ARRIVE, 1, 1, 0), (SPREAD, 7, 1, 0), (NORM, 0, 0, 0), (ARRIVE, 1, 1, 1), (SPREAD, 1, 1, 1),
-    (SPREAD, 7, 1, 1), (SPREAD, 1, 1, 0), (NORM, 0, 0, 0), (FORWARD, 1, 1, 1), (FORWARD, 7, 1, 0),
-    (FORWARD, 7, 1, 1), (ARRIVE, 1, 0, 0), (ARRIVE, 1, 0, 1), (FORWARD, 1, 1, 0), (ARRIVE, 2, 1, 0),
-    (SPREAD, 6, 1, 0), (ARRIVE, 2, 1, 1), (SPREAD, 2, 1, 0), (SPREAD, 2, 1, 1), (ARRIVE, 2, 0, 0),
-    (SPREAD, 6, 0, 0), (ARRIVE, 2, 0, 1), (SPREAD, 6, 0, 1), (NORM, 0, 0, 0), (NORM, 0, 0, 0),
-    (FORWARD, 6, 0, 0), (FORWARD, 2, 1, 0), (ARRIVE, 3, 1, 1), (SPREAD, 3, 1, 1), (ARRIVE, 3, 1, 0),
-    (FORWARD, 2, 1, 1), (FORWARD, 6, 0, 1), (ARRIVE, 3, 0, 0), (ARRIVE, 3, 0, 1), (SPREAD, 3, 0, 1),
-    (SPREAD, 3, 0, 0), (SPREAD, 5, 1, 1), (SPREAD, 5, 1, 0), (MULTIPLY, 1, 1, 0), (MULTIPLY, 6, 0, 0),
-    (ARRIVE, 4, 0, 1), (MULTIPLY, 2, 1, 0), (FORWARD, 3, 0, 0), (FORWARD, 3, 0, 1), (FORWARD, 5, 1, 1),
-    (MULTIPLY, 7, 1, 0), (FORWARD, 5, 1, 0), (ARRIVE, 4, 1, 0), (SPREAD, 5, 0, 0), (ARRIVE, 4, 1, 1),
-    (OWN, 0, 1, 0), (MULTIPLY, 3, 0, 0), (SPREAD, 4, 1, 0), (SPREAD, 5, 0, 1), (ARRIVE, 4, 0, 0),
-    (SPREAD, 4, 1, 1), (MULTIPLY, 5, 1, 0), (SPREAD, 3, 1, 0), (FORWARD, 4, 1, 0), (SPREAD, 6, 1, 1),
-    (FORWARD, 5, 0, 0), (FORWARD, 4, 1, 1), (FORWARD, 5, 0, 1), (FORWARD, 6, 1, 0), (FORWARD, 6, 1, 1),
-    (MULTIPLY, 4, 1, 0), (SPREAD, 4, 0, 1), (HAND_OVER, 1, 1, 0), (FORWARD, 3, 1, 0), (FORWARD, 3, 1, 1),
-    (MULTIPLY, 6, 1, 0), (SPREAD, 4, 0, 0), (FORWARD, 4, 0, 1), (SPREAD, 2, 0, 1), (MULTIPLY, 3, 1, 0),
-    (MULTIPLY, 5, 0, 0), (FORWARD, 4, 0, 0), (SPREAD, 2, 0, 0), (HAND_OVER, 7, 1, 0), (SPREAD, 1, 0, 0),
-    (MULTIPLY, 4, 0, 0), (HAND_OVER, 3, 1, 0), (FORWARD, 2, 0, 0), (FORWARD, 2, 0, 1), (SPREAD, 1, 0, 1),
-    (SPREAD, 7, 0, 1), (OWN, 0, 0, 0), (SPREAD, 7, 0, 0), (MULTIPLY, 2, 0, 0), (FORWARD, 1, 0, 0),
-    (HAND_OVER, 2, 1, 0), (FORWARD, 1, 0, 1), (FORWARD, 7, 0, 0), (FORWARD, 7, 0, 1), (HAND_OVER, 5, 1, 0),
-    (HAND_OVER, 4, 1, 0), (MULTIPLY, 1, 0, 0), (MULTIPLY, 7, 0, 0), (HAND_OVER, 6, 1, 0),
+    (NORM, 0, 0, 0), (ARRIVE, 1, 1, 0), (SPREAD, 7, 1, 0), (ARRIVE, 1, 1, 1), (SPREAD, 1, 1, 0),
+    (SPREAD, 7, 1, 1), (SPREAD, 1, 1, 1), (FORWARD, 1, 1, 0), (FORWARD, 7, 1, 0), (FORWARD, 7, 1, 1),
+    (ARRIVE, 1, 0, 1), (FORWARD, 1, 1, 1), (ARRIVE, 2, 1, 0), (SPREAD, 2, 1, 0), (NORM, 0, 0, 0),
+    (ARRIVE, 2, 1, 1), (SPREAD, 6, 1, 0), (NORM, 0, 0, 0), (SPREAD, 6, 1, 1), (ARRIVE, 1, 0, 0),
+    (NORM, 0, 0, 0), (SPREAD, 2, 1, 1), (ARRIVE, 2, 0, 1), (SPREAD, 6, 0, 1), (FORWARD, 2, 1, 1),
+    (ARRIVE, 3, 1, 0), (ARRIVE, 3, 1, 1), (SPREAD, 5, 1, 1), (ARRIVE, 2, 0, 0), (FORWARD, 2, 1, 0),
+    (SPREAD, 5, 1, 0), (ARRIVE, 3, 0, 1), (SPREAD, 3, 0, 1), (MULTIPLY, 7, 1, 0), (FORWARD, 5, 1, 0),
+    (FORWARD, 5, 1, 1), (MULTIPLY, 2, 1, 0), (ARRIVE, 3, 0, 0), (SPREAD, 3, 0, 0), (SPREAD, 6, 0, 0),
+    (MULTIPLY, 1, 1, 0), (ARRIVE, 4, 1, 1), (FORWARD, 3, 0, 1), (MULTIPLY, 5, 1, 0), (ARRIVE, 4, 1, 0),
+    (FORWARD, 6, 0, 1), (OWN, 0, 1, 0), (FORWARD, 3, 0, 0), (FORWARD, 6, 0, 0), (SPREAD, 4, 1, 1),
+    (ARRIVE, 4, 0, 1), (ARRIVE, 4, 0, 0), (SPREAD, 5, 0, 1), (SPREAD, 4, 1, 0), (SPREAD, 3, 1, 1),
+    (FORWARD, 6, 1, 0), (MULTIPLY, 3, 0, 0), (SPREAD, 4, 0, 1), (MULTIPLY, 6, 0, 0), (FORWARD, 6, 1, 1),
+    (FORWARD, 4, 1, 0), (OWN, 0, 0, 0), (SPREAD, 3, 1, 0), (FORWARD, 4, 1, 1), (SPREAD, 5, 0, 0),
+    (MULTIPLY, 6, 1, 0), (SPREAD, 4, 0, 0), (FORWARD, 3, 1, 1), (FORWARD, 3, 1, 0), (MULTIPLY, 4, 1, 0),
+    (FORWARD, 5, 0, 1), (FORWARD, 5, 0, 0), (SPREAD, 7, 0, 0), (MULTIPLY, 3, 1, 0), (HAND_OVER, 7, 1, 0),
+    (FORWARD, 4, 0, 0), (FORWARD, 4, 0, 1), (HAND_OVER, 1, 1, 0), (MULTIPLY, 5, 0, 0), (SPREAD, 2, 0, 1),
+    (SPREAD, 2, 0, 0), (MULTIPLY, 4, 0, 0), (SPREAD, 1, 0, 1), (FORWARD, 2, 0, 0), (FORWARD, 2, 0, 1),
+    (SPREAD, 1, 0, 0), (SPREAD, 7, 0, 1), (MULTIPLY, 2, 0, 0), (FORWARD, 1, 0, 1), (FORWARD, 1, 0, 0),
+    (HAND_OVER, 6, 1, 0), (HAND_OVER, 4, 1, 0), (FORWARD, 7, 0, 1), (FORWARD, 7, 0, 0), (MULTIPLY, 1, 0, 0),
+    (MULTIPLY, 7, 0, 0), (HAND_OVER, 5, 1, 0), (HAND_OVER, 3, 1, 0), (HAND_OVER, 2, 1, 0),
 )
 
 
@@ -142,8 +142,7 @@
         back = hop if direction == 0 else ring - hop
         block = (z + ring - back) % ring
         reference = part(block, HALVES * quarter + half)[kind]
-        landed = (hop + 1) if direction == 0 else ring - hop - 1
-        copy = remote(reference, reference, send_sem.at[kind], z_recv.at[(landed * HALVES + half) * 2 + kind], at_ring(ring - 1 if direction == 0 else 1))
+        copy = remote(reference, reference, send_sem.at[kind], z_recv.at[(hop * HALVES + half) * 2 + kind], at_ring(ring - 1 if direction == 0 else 1))
         copy.start()
 
     def reach(direction, half):
@@ -155,31 +154,26 @@
             landed = 1 if direction == 0 else ring - 1
             for core, source in enumerate((wk_hbm, wv_hbm)):
                 device = (dp, CORES * ((z + landed) % ring) + core)
-                remote(source.at[:, span], wkv.at[z, chunk, own_half], send_sem.at[1], z_recv.at[(landed * HALVES + half) * 2 + 1], device).start()
+                remote(source.at[:, span], wkv.at[z, chunk, own_half], send_sem.at[1], z_recv.at[half * 2 + 1], device).start()
 
     def query_start(half):
         span = pl.ds(pl.multiple_of((HALVES * quarter + half) * step, step), step)
         for direction in range(2):
             landed = 1 if direction == 0 else ring - 1
-            remote(wq_hbm.at[span], wq.at[z, span], send_sem.at[0], z_recv.at[(landed * HALVES + half) * 2], at_ring(ring - landed)).start()
-
-    def ring_arrival(direction, hop, half, kind):
-        back = hop if direction == 0 else ring - hop
-        block = (z + ring - back) % ring
-        reference = part(block, HALVES * quarter + half)[kind]
-        remote(reference, reference, send_sem.at[kind], z_recv.at[(back * HALVES + half) * 2 + kind], at_ring(1)).wait_recv()
+            remote(wq_hbm.at[span], wq.at[z, span], send_sem.at[0], z_recv.at[half * 2], at_ring(ring - landed)).start()
 
     def ring_service(hop, kind, half):
-        for direction in range(2):
-            if hop <= reach(direction, half):
-                ring_arrival(direction, hop, half, kind)
-                if hop < reach(direction, half):
-                    ring_send(direction, hop, half, kind)
+        directions = [d for d in range(2) if hop <= reach(d, half)]
+        arrived = (wq.at[0, pl.ds(0, len(directions) * step)], wkv.at[0, pl.ds(0, len(directions))])[kind]
+        remote(arrived, arrived, send_sem.at[kind], z_recv.at[((hop - 1) * HALVES + half) * 2 + kind], partner).wait_recv()
+        for direction in directions:
+            if hop < reach(direction, half):
+                ring_send(direction, hop, half, kind)
 
     def square_copy(r, lane_index, chunk, kind, device):
         block = (z + ring - r) % ring
         reference = part(block, chunk)[kind]
-        index = (r * 3 + {0: 0, 3: 1}.get(lane_index, 2)) * 2 + kind
+        index = ((r - 1) * 3 + {0: 0, 3: 1}.get(lane_index, 2)) * 2 + kind
         return remote(reference, reference, send_sem.at[kind], xy_recv.at[index], device)
 
     def square_send(r, kind, half):
@@ -194,7 +188,7 @@
     def square_rest(r, kind):
         block = (z + ring - r) % ring
         four = (wq.at[block, pl.ds(0, 4 * step)], wkv.at[block, pl.ds(0, 4)])[kind]
-        remote(four, four, send_sem.at[kind], xy_recv.at[(r * 3 + 2) * 2 + kind], x_peer).wait_recv()
+        remote(four, four, send_sem.at[kind], xy_recv.at[((r - 1) * 3 + 2) * 2 + kind], x_peer).wait_recv()
 
     def flatten(block):
         @pl.loop(0, CHUNKS)
@@ -220,7 +214,7 @@
         span, target = pl.ds(first, count), out_rows(z, first, count)
         if kind == 0:
             return remote(oq.at[r, span], q_out.at[target], send_sem.at[PRODUCTS], recv_sem.at[0], at_ring(r))
-        return remote(okv.at[r, span], kv_out.at[c, target], send_sem.at[PRODUCTS + 1], okv_recv.at[r], at_ring(r))
+        return remote(okv.at[r, span], kv_out.at[c, target], send_sem.at[PRODUCTS + 1], okv_recv.at[r - 1], at_ring(r))
 
     def multiply(r, kind):
         block = (z + ring - r) % ring
@@ -245,7 +239,7 @@
 
     def relay(r):
         target = out_rows((z + r) % ring, 0, chip_rows)
-        remote(okv.at[r], kv_out.at[c, target], send_sem.at[PRODUCTS + 1], okv_recv.at[r], at_ring(r)).wait_recv()
+        remote(okv.at[r], kv_out.at[c, target], send_sem.at[PRODUCTS + 1], okv_recv.at[r - 1], at_ring(r)).wait_recv()
         hand_over(r, kv_out.at[c, target]).start()
 
     for half in range(HALVES):
@@ -368,7 +362,7 @@
                 pltpu.VMEM((ring, chip_rows, heads, width), bf16),
                 pltpu.VMEM((ring, chip_rows, width), bf16),
                 dma((8,)), dma((HANDED + 1,)), dma((4,)),
-                dma((ring * HALVES * 2,)), dma((ring * 3 * 2,)), dma((ring,)), dma((2,)),
+                dma((ring // 2 * HALVES * 2,)), dma(((ring - 1) * 3 * 2,)), dma((ring - 1,)), dma((2,)),
             ],
             compiler_params=pltpu.CompilerParams(collective_id=0, has_side_effects=True, vmem_limit_bytes=42 * 1024 * 1024),
         )(*(pltpu.with_memory_space_constraint(a, pltpu.HBM) for a in (x_rows, norm_gain.reshape(1, depth), w_q, w_k.T, w_v.T)))

time: 214 us -> 213 us (level); the launches traced: 212 us -> 213 us
  no operation moved by 1% of the time
where the time goes in v5:
time: 213 us
  Pallas kernels  213 us (100%)
    pallas_call x1, Pallas kernels, local_step(): pl.pallas_call(functools.partial(kernel, ring, side), out_shape=(jax.Shap...  209 us

profile of v5, /device:TPU:22, one launch (start us, length us, event | category | flops | bytes accessed | tf_op | source)
XLA Modules:
  0.0 213.3 jit_solution(234240261315949749)
XLA Ops:
  0.6 209.3 %shard_map.76 = (bf16[8192,2,128]{2,1,0:T(2,128)(2,1)S(1)}, bf16[2,8192,128]{2,1,0:T(8,128)(2,1)S(1)}) custom-call(bf16[512,4096]{1,0:T(8,128)(2,1)} %x_hbm.1, f32[1,4096]{1,0:T(1,128)} %bitcast.7, bf16[4096,2,128]{2,1,0:T(2,128)(2,1)} %wq_hbm.1, bf16[64,4096]{1,0:T(8,128)(2,1)} %bitcast.5, bf16[64,4096]{1,0:T(8,128)(2,1)} %bitcast.6), custom_call_target="tpu_custom_call" | custom-call | tf_op jit(solution)/shard_map/pallas_call | solution.py:348
  209.9 3.4 %shard_map.77 = (bf16[8192,2,128]{2,1,0:T(2,128)(2,1)}, bf16[8192,128]{1,0:T(8,128)(2,1)}, bf16[8192,128]{1,0:T(8,128)(2,1)}) custom-call(bf16[8192,2,128]{2,1,0:T(2,128)(2,1)S(1)} %get-tuple-element.8.q_ref, bf16[2,8192,128]{2,1,0:T(8,128)(2,1)S(1)} %get-tuple-element.9.kv_ref), custom_call_target="tpu_custom_call" | custom-call | tf_op jit(solution)/shard_map/pallas_call | solution.py:370

commit v6 on v5

--- a/solution.py
+++ b/solution.py
@@ -105,23 +105,9 @@
         pieces = wkv.at[z, :, own_half]
         remote(pieces, pieces, send_sem.at[PAIRS], recv_sem.at[3], partner).wait_recv()
 
-    w_loads[0].start()
     for load in x_loads:
         load.start()
     gain_load.start()
-
-    @pl.when(c == 0)
-    def _():
-        for i in range(CHUNKS):
-            pair_load(wk_hbm, i).start()
-
-    @pl.when(c == 1)
-    def _():
-        for i in range(CHUNKS):
-            pair_load(wv_hbm, i).start()
-
-    for load in w_loads[1:]:
-        load.start()
 
     pl.semaphore_wait(barrier, len(peers))
 
@@ -246,6 +232,19 @@
         key_value_start(half)
     for half in range(HALVES):
         query_start(half)
+    @pl.when(c == 0)
+    def _():
+        for i in range(CHUNKS):
+            pair_load(wk_hbm, i).start()
+
+    @pl.when(c == 1)
+    def _():
+        for i in range(CHUNKS):
+            pair_load(wv_hbm, i).start()
+
+    for load in w_loads:
+        load.start()
+
     pair_start()
     for i in range(CHUNKS):
         pair_load(wk_hbm, i).wait()

time: 213 us -> 213 us (level)
  no operation moved by 1% of the time
where the time goes in v6:
time: 213 us
  Pallas kernels  213 us (100%)
    pallas_call x1, Pallas kernels, local_step(): pl.pallas_call(functools.partial(kernel, ring, side), out_shape=(jax.Shap...  209 us

profile of v6, /device:TPU:22, one launch (start us, length us, event | category | flops | bytes accessed | tf_op | source)
XLA Modules:
  0.0 213.2 jit_solution(11040631319303187071)
XLA Ops:
  0.6 209.2 %shard_map.76 = (bf16[8192,2,128]{2,1,0:T(2,128)(2,1)S(1)}, bf16[2,8192,128]{2,1,0:T(8,128)(2,1)S(1)}) custom-call(bf16[512,4096]{1,0:T(8,128)(2,1)} %x_hbm.1, f32[1,4096]{1,0:T(1,128)} %bitcast.7, bf16[4096,2,128]{2,1,0:T(2,128)(2,1)} %wq_hbm.1, bf16[64,4096]{1,0:T(8,128)(2,1)} %bitcast.5, bf16[64,4096]{1,0:T(8,128)(2,1)} %bitcast.6), custom_call_target="tpu_custom_call" | custom-call | tf_op jit(solution)/shard_map/pallas_call | solution.py:347
  209.8 3.4 %shard_map.77 = (bf16[8192,2,128]{2,1,0:T(2,128)(2,1)}, bf16[8192,128]{1,0:T(8,128)(2,1)}, bf16[8192,128]{1,0:T(8,128)(2,1)}) custom-call(bf16[8192,2,128]{2,1,0:T(2,128)(2,1)S(1)} %get-tuple-element.8.q_ref, bf16[2,8192,128]{2,1,0:T(8,128)(2,1)S(1)} %get-tuple-element.9.kv_ref), custom_call_target="tpu_custom_call" | custom-call | tf_op jit(solution)/shard_map/pallas_call | solution.py:369
